TPU v7x, 16 devices: a whole 2x2x2 slice. The times are simulated.
16 devices in a mesh: tp: 2 (over z), fsdp: 8 (over y, x, core).
Axes of the slice: x: 2, y: 2, z: 2, core: 2. Of those that a mesh axis runs over, the one named last changes fastest.
Arguments:
- x_in: bfloat16 [24, 1024, 2048], P('fsdp')
- dy_out: bfloat16 [24, 1024, 2048], P('fsdp')
- ln_gain: float32 [2048], P('fsdp')
- w_q: bfloat16 [2048, 2048], P('fsdp', 'tp')
- w_k: bfloat16 [2048, 128], P('fsdp')
- w_v: bfloat16 [2048, 128], P('fsdp')
- w_o: bfloat16 [2048, 2048], P('tp', 'fsdp')
- w_gate: bfloat16 [2048, 8192], P('fsdp', 'tp')
- w_up: bfloat16 [2048, 8192], P('fsdp', 'tp')
- w_down: bfloat16 [8192, 2048], P('tp', 'fsdp')
Outputs:
- output 1: bfloat16 [24, 1024, 2048], P('fsdp')
- output 2: bfloat16 [24, 1024, 2048], P('fsdp')
- output 3: float32 [2048], P('fsdp')
- output 4: float32 [2048, 2048], P('fsdp', 'tp')
- output 5: float32 [2048, 128], P('fsdp')
- output 6: float32 [2048, 128], P('fsdp')
- output 7: float32 [2048, 2048], P('tp', 'fsdp')
- output 8: float32 [2048, 8192], P('fsdp', 'tp')
- output 9: float32 [2048, 8192], P('fsdp', 'tp')
- output 10: float32 [8192, 2048], P('tp', 'fsdp')
All inputs are finite; a program needn't handle non-finite values.
Results may differ from a plain program's by a relative error of at most 0.0155669.
Values are sent between devices in bfloat16 or wider.
A program may use at most 1 GiB of HBM per device.

v0:
```python
import math
import jax
import jax.numpy as jnp
from jax import lax
from jax.sharding import PartitionSpec as P


def layer_norm(x_f32, gain):
    x_mean = jnp.mean(x_f32, axis=-1, keepdims=True)
    x_cent = x_f32 - x_mean
    x_var = jnp.mean(x_cent * x_cent, axis=-1, keepdims=True)
    return (x_cent * lax.rsqrt(x_var + 1e-5) * gain).astype(jnp.bfloat16)


def rotate(vals, cos_t, sin_t):
    half_dim = vals.shape[-1] // 2
    first = vals[..., :half_dim]
    second = vals[..., half_dim:]
    return jnp.concatenate([first * cos_t - second * sin_t, second * cos_t + first * sin_t], axis=-1)


def qk_post(q_raw, k_raw):
    seq_len = k_raw.shape[1]
    head_dim = k_raw.shape[2]
    half_dim = head_dim // 2
    inv_freq = jnp.power(10000.0, -2.0 * jnp.arange(half_dim, dtype=jnp.float32) / head_dim)
    angle = jnp.arange(seq_len, dtype=jnp.float32)[:, None] * inv_freq[None, :]
    cos_t = jnp.cos(angle)
    sin_t = jnp.sin(angle)
    q_rot = rotate(q_raw.astype(jnp.float32), cos_t[:, None, :], sin_t[:, None, :]) * (1.0 / math.sqrt(head_dim))
    k_rot = rotate(k_raw.astype(jnp.float32), cos_t, sin_t)
    return q_rot.astype(jnp.bfloat16), k_rot.astype(jnp.bfloat16)


def attend(q_rot, k_rot, v_val):
    seq_len = q_rot.shape[1]
    causal = lax.broadcasted_iota(jnp.int32, (seq_len, 1, seq_len), 0) >= lax.broadcasted_iota(jnp.int32, (seq_len, 1, seq_len), 2)
    scores = jnp.einsum('crie,cle->cril', q_rot, k_rot, preferred_element_type=jnp.float32)
    scores = jnp.where(causal, scores, -1e30)
    row_max = lax.stop_gradient(jnp.max(scores, axis=-1, keepdims=True))
    exp_val = jnp.exp(scores - row_max)
    att_prob = (exp_val / jnp.sum(exp_val, axis=-1, keepdims=True)).astype(jnp.bfloat16)
    return jnp.einsum('cril,cle->crie', att_prob, v_val, preferred_element_type=jnp.float32).astype(jnp.bfloat16)


def swiglu(gate_val, up_val):
    return (jax.nn.silu(gate_val.astype(jnp.float32)) * up_val.astype(jnp.float32)).astype(jnp.bfloat16)


def matmul_f32(form, left, right):
    return jnp.einsum(form, left, right, preferred_element_type=jnp.float32)


def gather_rows(w_part):
    return lax.all_gather(w_part, 'fsdp', axis=0, tiled=True)


def gather_cols(w_part):
    return lax.all_gather(w_part, 'fsdp', axis=1, tiled=True)


def scatter_rows(grad_full):
    return lax.psum_scatter(grad_full, 'fsdp', scatter_dimension=0, tiled=True)


def scatter_cols(grad_full):
    return lax.psum_scatter(grad_full, 'fsdp', scatter_dimension=1, tiled=True)


def solution(mesh):
    def device_step(x_in, dy_out, ln_gain, w_q, w_k, w_v, w_o, w_gate, w_up, w_down):
        n_batch, seq_len, _ = x_in.shape
        head_dim = w_k.shape[1]
        gain_full = lax.all_gather(ln_gain, 'fsdp', tiled=True)
        x_f32 = x_in.astype(jnp.float32)
        h_norm, norm_pull = jax.vjp(layer_norm, x_f32, gain_full)
        wq_full = gather_rows(w_q)
        wk_full = gather_rows(w_k)
        wv_full = gather_rows(w_v)
        wg_full = gather_rows(w_gate)
        wu_full = gather_rows(w_up)
        q_raw = matmul_f32('bsd,de->bse', h_norm, wq_full).astype(jnp.bfloat16)
        k_raw = matmul_f32('bsd,de->bse', h_norm, wk_full).astype(jnp.bfloat16)
        v_val = matmul_f32('bsd,de->bse', h_norm, wv_full).astype(jnp.bfloat16)
        gate_val = matmul_f32('bsd,df->bsf', h_norm, wg_full).astype(jnp.bfloat16)
        up_val = matmul_f32('bsd,df->bsf', h_norm, wu_full).astype(jnp.bfloat16)
        q_heads = q_raw.reshape(n_batch, seq_len, -1, head_dim)
        (q_rot, k_rot), rope_pull = jax.vjp(qk_post, q_heads, k_raw)
        att_out, att_pull = jax.vjp(attend, q_rot, k_rot, v_val)
        mlp_act, act_pull = jax.vjp(swiglu, gate_val, up_val)
        att_flat = att_out.reshape(n_batch, seq_len, -1)
        wo_full = gather_cols(w_o)
        wd_full = gather_cols(w_down)
        branch_part = (matmul_f32('bse,ed->bsd', att_flat, wo_full) + matmul_f32('bsf,fd->bsd', mlp_act, wd_full)).astype(jnp.bfloat16)
        branch_sum = lax.psum(branch_part, 'tp')
        y_out = (x_f32 + branch_sum.astype(jnp.float32)).astype(jnp.bfloat16)

        wo_back = gather_cols(w_o)
        wd_back = gather_cols(w_down)
        grad_wo = scatter_cols(matmul_f32('bse,bsd->ed', att_flat, dy_out))
        grad_wdown = scatter_cols(matmul_f32('bsf,bsd->fd', mlp_act, dy_out))
        d_att = matmul_f32('bsd,ed->bse', dy_out, wo_back).astype(jnp.bfloat16).reshape(n_batch, seq_len, -1, head_dim)
        d_act = matmul_f32('bsd,fd->bsf', dy_out, wd_back).astype(jnp.bfloat16)
        d_gate, d_up = act_pull(d_act)
        d_qrot, dk_part, dv_part = att_pull(d_att)
        kv_sum = lax.psum(jnp.concatenate([dk_part, dv_part], axis=-1).astype(jnp.float32), 'tp')
        d_krot = kv_sum[..., :head_dim].astype(jnp.bfloat16)
        d_val = kv_sum[..., head_dim:].astype(jnp.bfloat16)
        d_qraw, d_kraw = rope_pull((d_qrot, d_krot))
        d_qflat = d_qraw.reshape(n_batch, seq_len, -1)
        grad_wq = scatter_rows(matmul_f32('bsd,bse->de', h_norm, d_qflat))
        grad_wk = scatter_rows(matmul_f32('bsd,bse->de', h_norm, d_kraw))
        grad_wv = scatter_rows(matmul_f32('bsd,bse->de', h_norm, d_val))
        grad_wgate = scatter_rows(matmul_f32('bsd,bsf->df', h_norm, d_gate))
        grad_wup = scatter_rows(matmul_f32('bsd,bsf->df', h_norm, d_up))
        wq_back = gather_rows(w_q)
        wk_back = gather_rows(w_k)
        wv_back = gather_rows(w_v)
        wg_back = gather_rows(w_gate)
        wu_back = gather_rows(w_up)
        dh_part = (matmul_f32('bse,de->bsd', d_qflat, wq_back) + matmul_f32('bsf,df->bsd', d_gate, wg_back) + matmul_f32('bsf,df->bsd', d_up, wu_back)).astype(jnp.bfloat16)
        dh_sum = lax.psum(dh_part, 'tp')
        dh_full = (dh_sum.astype(jnp.float32) + matmul_f32('bse,de->bsd', d_kraw, wk_back) + matmul_f32('bse,de->bsd', d_val, wv_back)).astype(jnp.bfloat16)
        dx_norm, gain_part = norm_pull(dh_full)
        grad_x = (dy_out.astype(jnp.float32) + dx_norm).astype(jnp.bfloat16)
        grad_gain = lax.psum_scatter(gain_part, 'fsdp', scatter_dimension=0, tiled=True)
        return (y_out, grad_x, grad_gain, grad_wq, grad_wk, grad_wv, grad_wo, grad_wgate, grad_wup, grad_wdown)

    act_spec = P('fsdp', None, None)
    row_spec = P('fsdp', 'tp')
    kv_spec = P('fsdp', None)
    col_spec = P('tp', 'fsdp')
    in_specs = (act_spec, act_spec, P('fsdp'), row_spec, kv_spec, kv_spec, col_spec, row_spec, row_spec, col_spec)
    out_specs = (act_spec, act_spec, P('fsdp'), row_spec, kv_spec, kv_spec, col_spec, row_spec, row_spec, col_spec)
    return jax.shard_map(device_step, mesh=mesh, in_specs=in_specs, out_specs=out_specs, check_vma=False)
```

profile of v0, /device:TPU:0, one launch (start us, length us, event | category | flops | bytes accessed | tf_op | source)
XLA Modules:
  0.0 2299.3 jit_solution(4666459585318892955)
XLA Ops:
  7.2 2.0 copy.79
  9.4 0.7 all-gather.9.cloned.1.call-update
  10.1 0.7 all-gather.15.cloned.1.call-update
  10.8 0.5 all-gather.13.cloned.1.call-update
  11.4 0.5 all-gather.11.cloned.1.call-update
  12.3 10.8 all-gather
  23.1 6.3 convert_reduce_fusion
  29.5 8.7 fusion.27
  38.1 0.6 copy-done.25
  38.9 12.9 all_gather.33
  51.8 1.0 fusion.77
  53.2 11.1 all_gather.34
  64.3 8.3 fusion.68
  72.6 8.0 fusion.67
  80.7 1.0 subtract_convert_fusion
  81.7 17.9 fusion.61
  99.6 6.2 fusion.100
  105.8 9.5 copy.145
  115.4 9.9 copy.144
  125.3 15.3 multiply_subtract_fusion
  140.6 9.6 fusion.52
  150.2 42.6 %fusion.101 = (f32[3,1024,8]{1,2,0:T(8,128)S(1)}, f32[3,1024,8,1024]{1,3,2,0:T(8,128)}) fusion(pred[1024,1024]{0,1:T(8,128)(4,1)S(1)} %iota_compare_fusion, bf16[3,1024,8,128]{3,1,2,0:T(8,128)(2,1)} %fusion.52, bf16[3,1024,64]{1,2,0:T(8,128)(2,1)S(1)} %copy-done.21, bf16[3,1024,64]{1,2,0:T(8,128)(2,1)S(1)} %get-tuple-element.29), kind=kOutput, calls=%fused_computation.132 | convolution fusion | flops 6519522304 | bytes 108888064 | tf_op jit(solution)/shard_map/jvp()/sub | solution.py:41
  192.8 18.5 fusion.64
  211.3 73.3 %fusion.5 = (f32[3,1024,8]{1,2,0:T(8,128)S(1)}, bf16[3,1024,8,1024]{1,3,2,0:T(8,128)(2,1)}, bf16[3,1024,8,1024]{1,3,2,0:T(8,128)(2,1)}) fusion(f32[3,1024,8,1024]{1,3,2,0:T(8,128)} %get-tuple-element.34, f32[3,1024,8]{1,2,0:T(8,128)S(1)} %multiply_divide_fusion, f32[3,1024,8]{1,2,0:T(8,128)S(1)} %get-tuple-element.33, ...), kind=kOutput, calls=%fused_computation.7 | convolution fusion | flops 6618587136 | bytes 208699392 | tf_op jit(solution)/shard_map/transpose(jvp(cril,cle->crie))/dot_general | solution.py:43
  284.6 56.1 %convert_multiply_fusion.8 = f32[3,1024,8,128]{3,1,2,0:T(8,128)} fusion(bf16[3,1024,64]{1,2,0:T(8,128)(2,1)S(1)} %copy-done.21, bf16[3,1024,64]{1,2,0:T(8,128)(2,1)S(1)} %get-tuple-element.29, f32[3,1024,8,1024]{1,3,2,0:T(8,128)} %get-tuple-element.34, bf16[3,1024,8,1024]{1,3,2,0:T(8,128)(2,1)} %get-tuple-element.35, f32[3,1024,8]{1,2,0:T(8,128)S(1)} %neg.20, ...), kind=kOutput, calls=%fused_computation.75 | convolution fusion | flops 6579290112 | bytes 165609472 | tf_op jit(solution)/shard_map/transpose(jvp(crie,cle->cril))/dot_general | solution.py:38
  340.8 16.4 multiply_add_fusion.1
  357.2 9.6 add_convert_fusion.4
  366.8 8.7 copy.92
  375.5 20.4 convolution_convert_fusion.1
  396.0 61.3 %fusion.49 = bf16[3,1024,4096]{2,1,0:T(8,128)(2,1)} fusion(bf16[3,1024,2048]{2,1,0:T(8,128)(2,1)} %param.11, bf16[4096,2048]{1,0:T(8,128)(2,1)} %all-gather.15.cloned.1.call-done), kind=kOutput, calls=%fused_computation.69 | convolution fusion | flops 51552190464 | bytes 54525952 | tf_op jit(solution)/shard_map/bsd,fd->bsf/dot_general | solution.py:51
  457.3 60.6 %fusion.46 = bf16[3,1024,4096]{2,1,0:T(8,128)(2,1)} fusion(bf16[2048,4096]{1,0:T(8,128)(2,1)} %all-gather.13.cloned.1.call-done, bf16[3,1024,2048]{2,1,0:T(8,128)(2,1)} %param.10, f32[2048]{0:T(1024)S(1)} %bitcast.143, f32[3,1024]{1,0:T(4,128)S(1)} %copy-done.28, f32[3,1024]{1,0:T(4,128)S(1)} %copy-done.17), kind=kOutput, calls=%fused_computation.68 | convolution fusion | flops 51583647744 | bytes 54558720 | tf_op jit(solution)/shard_map/bsd,df->bsf/dot_general | solution.py:51
  517.8 94.4 %fusion.16 = (bf16[3,1024,4096]{2,1,0:T(8,128)(2,1)}, bf16[3,1024,4096]{2,1,0:T(8,128)(2,1)}, bf16[3,1024,4096]{2,1,0:T(8,128)(2,1)}) fusion(bf16[3,1024,4096]{2,1,0:T(8,128)(2,1)} %fusion.46, bf16[3,1024,4096]{2,1,0:T(8,128)(2,1)} %fusion.49, bf16[2048,4096]{1,0:T(8,128)(2,1)} %all-gather.11.cloned.1.call-done, bf16[3,1024,2048]{2,1,0:T(8,128)(2,1)} %param.10, ...), kind=kOutput, calls=%fused_computation.26 | convolution fusion | flops 51822723072 | bytes 155222016 | tf_op jit(solution)/shard_map/bsd,df->bsf/dot_general | solution.py:51
  612.3 61.2 %fusion.38 = f32[3,1024,2048]{2,1,0:T(8,128)} fusion(bf16[3,1024,4096]{2,1,0:T(8,128)(2,1)} %get-tuple-element.16, bf16[2048,4096]{1,0:T(8,128)(2,1)} %all-gather.11.cloned.1.call-done), kind=kOutput, calls=%fused_computation.62 | convolution fusion | flops 51539607552 | bytes 67108864 | tf_op jit(solution)/shard_map/bsf,df->bsd/dot_general | solution.py:51
  673.5 61.2 %fusion.34 = f32[3,1024,2048]{2,1,0:T(8,128)} fusion(bf16[3,1024,4096]{2,1,0:T(8,128)(2,1)} %get-tuple-element.17, bf16[2048,4096]{1,0:T(8,128)(2,1)} %all-gather.13.cloned.1.call-done), kind=kOutput, calls=%fused_computation.58 | convolution fusion | flops 51539607552 | bytes 67108864 | tf_op jit(solution)/shard_map/bsf,df->bsd/dot_general | solution.py:51
  734.7 61.2 %fusion.32 = f32[3,1024,2048]{2,1,0:T(8,128)} fusion(bf16[3,1024,4096]{2,1,0:T(8,128)(2,1)} %get-tuple-element.18, bf16[4096,2048]{1,0:T(8,128)(2,1)} %all-gather.15.cloned.1.call-done), kind=kOutput, calls=%fused_computation.56 | convolution fusion | flops 51539607552 | bytes 67108864 | tf_op jit(solution)/shard_map/bsf,fd->bsd/dot_general | solution.py:51
  795.9 23.1 %add_convert_fusion.3 = bf16[3,1024,2048]{2,1,0:T(8,128)(2,1)} fusion(f32[3,1024,2048]{2,1,0:T(8,128)} %fusion.32, bf16[3,1024,1024]{1,2,0:T(8,128)(2,1)} %bitcast.134, bf16[1024,2048]{1,0:T(8,128)(2,1)} %all-gather.9.cloned.1.call-done), kind=kOutput, calls=%fused_computation.50 | convolution fusion | flops 12897484800 | bytes 48234496 | tf_op jit(solution)/shard_map/bse,ed->bsd/dot_general | solution.py:51
  819.0 30.7 %add_convert_fusion.2 = bf16[3,1024,2048]{2,1,0:T(8,128)(2,1)} fusion(f32[3,1024,2048]{2,1,0:T(8,128)} %fusion.34, f32[3,1024,2048]{2,1,0:T(8,128)} %fusion.38, bf16[3,1024,1024]{1,2,0:T(8,128)(2,1)} %bitcast.138, bf16[2048,1024]{0,1:T(8,128)(2,1)} %all-gather.7.cloned.1.call-done), kind=kOutput, calls=%fused_computation.49 | convolution fusion | flops 12903776256 | bytes 73400320 | tf_op jit(solution)/shard_map/bse,de->bsd/dot_general | solution.py:51
  849.9 26.7 %bitcast_convert_fusion = bf16[3,1024,128]{1,2,0:T(8,128)(2,1)} fusion(bf16[3,1024,8,1024]{1,3,2,0:T(8,128)(2,1)} %get-tuple-element.15, bf16[3,1024,8,128]{1,3,2,0:T(8,128)(2,1)} %bitcast.137), kind=kOutput, calls=%fused_computation.94 | convolution fusion | flops 6442844160 | bytes 57409536 | tf_op jit(solution)/shard_map/transpose(jvp(cril,cle->crie))/dot_general | solution.py:43
  876.6 52.0 %bitcast_convert_fusion.1 = bf16[3,1024,128]{1,2,0:T(8,128)(2,1)} fusion(bf16[3,1024,8,128]{3,1,2,0:T(8,128)(2,1)} %fusion.52, f32[3,1024,8,1024]{1,3,2,0:T(8,128)} %get-tuple-element.34, bf16[3,1024,8,1024]{1,3,2,0:T(8,128)(2,1)} %get-tuple-element.35, f32[3,1024,8]{1,2,0:T(8,128)S(1)} %copy-done.33, f32[3,1024,8]{1,2,0:T(8,128)S(1)} %copy-done.31, ...), kind=kOutput, calls=%fused_computation.95 | convolution fusion | flops 6568673280 | bytes 159318016 | tf_op jit(solution)/shard_map/transpose(jvp(crie,cle->cril))/dot_general | solution.py:38
  928.6 1.8 maximum_convert_fusion
  930.4 146.0 %all-reduce.10 = bf16[3,1024,256]{1,2,0:T(8,128)(2,1)} all-reduce(f32[3,1024,256]{1,2,0:T(8,128)S(1)} %maximum_convert_fusion), channel_id=1, replica_groups=mesh['tp'=2,'fsdp'=8] {'tp'}, use_global_device_ids=true, to_apply=%region_7.8 | all-reduce | flops 786432 | bytes 4718592 | tf_op jit(solution)/shard_map/psum | solution.py:106
  1076.4 1.3 slice_convert_fusion
  1077.8 1.2 multiply_add_fusion.4
  1079.0 11.7 convolution_bitcast_fusion.5
  1090.8 10.0 convolution_bitcast_fusion.6
  1100.9 18.8 convolution_bitcast_fusion.4
  1119.8 21.8 convolution_bitcast_fusion.3
  1141.7 68.5 %convolution_bitcast_fusion.1 = f32[2048,4096]{1,0:T(8,128)} fusion(bf16[3,1024,4096]{2,1,0:T(8,128)(2,1)} %get-tuple-element.16, bf16[3,1024,2048]{2,1,0:T(8,128)(2,1)} %param.10, f32[2048]{0:T(1024)S(1)} %bitcast.148, f32[3,1024]{1,0:T(4,128)S(1)} %copy-done.29, f32[3,1024]{1,0:T(4,128)S(1)} %copy-done.18), kind=kOutput, calls=%fused_computation.52 | convolution fusion | flops 51571064832 | bytes 71335936 | tf_op jit(solution)/shard_map/bsd,bsf->df/dot_general | solution.py:51
  1210.2 69.1 %convolution_bitcast_fusion = f32[2048,4096]{1,0:T(8,128)} fusion(bf16[3,1024,4096]{2,1,0:T(8,128)(2,1)} %get-tuple-element.17, bf16[3,1024,2048]{2,1,0:T(8,128)(2,1)} %param.10, f32[2048]{0:T(1024)S(1)} %bitcast.149, f32[3,1024]{1,0:T(4,128)S(1)} %copy-done.29, f32[3,1024]{1,0:T(4,128)S(1)} %copy-done.18), kind=kOutput, calls=%fused_computation.51 | convolution fusion | flops 51571064832 | bytes 71335936 | tf_op jit(solution)/shard_map/bsd,bsf->df/dot_general | solution.py:51
  1279.4 63.5 %convolution_bitcast_fusion.2 = f32[4096,2048]{1,0:T(8,128)} fusion(bf16[3,1024,4096]{2,1,0:T(8,128)(2,1)} %get-tuple-element.18, bf16[3,1024,2048]{2,1,0:T(8,128)(2,1)} %param.11), kind=kOutput, calls=%fused_computation.53 | convolution fusion | flops 51539607552 | bytes 71303168 | tf_op jit(solution)/shard_map/bsf,bsd->fd/dot_general | solution.py:51
  1343.0 0.6 copy-done.36
  1343.6 0.6 dynamic-slice
  1344.8 11.5 fusion.73
  1356.3 115.5 %all-reduce.9.cloned.1.call-done = (bf16[3,1024,2048]{2,1,0:T(8,128)(2,1)}, bf16[3,1024,2048]{2,1,0:T(8,128)(2,1)}) async-done(((bf16[3,1024,2048]{2,1,0:T(8,128)(2,1)}, bf16[3,1024,2048]{2,1,0:T(8,128)(2,1)}), (bf16[3,1024,2048]{2,1,0:T(8,128)(2,1)}, bf16[3,1024,2048]{2,1,0:T(8,128)(2,1)})) %all-reduce.9.cloned.1.call-update) | async-done | bytes 25165840 | tf_op jit(solution)/shard_map/psum | solution.py:95
  1471.8 24.4 %fusion.28 = (f32[3,1024]{1,0:T(4,128)S(1)}, bf16[3,1024,2048]{2,1,0:T(8,128)(2,1)}) fusion(bf16[3,1024,2048]{2,1,0:T(8,128)(2,1)} %param.10, f32[2048]{0:T(1024)S(1)} %bitcast.150, f32[3,1024]{1,0:T(4,128)S(1)} %copy-done.18, bf16[2048,128]{1,0:T(8,128)(2,1)} %copy-done.12, bf16[3,1024,256]{1,2,0:T(8,128)(2,1)S(1)} %copy-done, ...), kind=kOutput, calls=%fused_computation.45 | convolution fusion | flops 1673524224 | bytes 64262144 | tf_op jit(solution)/shard_map/bse,de->bsd/dot_general | solution.py:51
  1496.2 14.9 fusion.26
  1511.1 13.8 all-reduce.4
  1525.0 0.6 dynamic-slice.1
  1525.6 28.3 %add_convert_fusion = (bf16[3,1024,2048]{2,1,0:T(8,128)(2,1)}, bf16[3,1024,2048]{2,1,0:T(8,128)(2,1)}) fusion(bf16[3,1024,2048]{2,1,0:T(8,128)(2,1)} %param.11, bf16[3,1024,2048]{2,1,0:T(8,128)(2,1)} %param.10, bf16[3,1024,2048]{2,1,0:T(8,128)(2,1)} %get-tuple-element.37, f32[3,1024]{1,0:T(4,128)S(1)} %negate_multiply_fusion, ...), kind=kLoop, calls=%fused_computation.47 | loop fusion | flops 94371840 | bytes 75554816 | tf_op jit(solution)/shard_map/convert_element_type | solution.py:125
  1554.0 57.1 %reduce-scatter.14.cloned.1.call-done = f32[1024,256]{1,0:T(8,128)} async-done(((f32[1024,2048]{1,0:T(8,128)}), f32[1024,256]{1,0:T(8,128)}) %reduce-scatter.14.cloned.1.call-update) | async-done | bytes 1048592 | tf_op jit(solution)/shard_map/reduce_scatter | solution.py:67
  1611.1 69.8 %reduce-scatter.8.cloned.1.call-done = f32[256,1024]{1,0:T(8,128)} async-done(((f32[2048,1024]{1,0:T(8,128)}), f32[256,1024]{1,0:T(8,128)}) %reduce-scatter.8.cloned.1.call-update) | async-done | bytes 1048592 | tf_op jit(solution)/shard_map/reduce_scatter | solution.py:63
  1680.9 204.0 %reduce-scatter.16.cloned.1.call-done = f32[256,4096]{1,0:T(8,128)} async-done(((f32[2048,4096]{1,0:T(8,128)}), f32[256,4096]{1,0:T(8,128)}) %reduce-scatter.16.cloned.1.call-update) | async-done | bytes 4194320 | tf_op jit(solution)/shard_map/reduce_scatter | solution.py:63
  1884.9 203.9 %reduce-scatter.18.cloned.1.call-done = f32[256,4096]{1,0:T(8,128)} async-done(((f32[2048,4096]{1,0:T(8,128)}), f32[256,4096]{1,0:T(8,128)}) %reduce-scatter.18.cloned.1.call-update) | async-done | bytes 4194320 | tf_op jit(solution)/shard_map/reduce_scatter | solution.py:63
  2088.7 203.8 %reduce-scatter.20.cloned.1.call-done = f32[4096,256]{1,0:T(8,128)} async-done(((f32[4096,2048]{1,0:T(8,128)}), f32[4096,256]{1,0:T(8,128)}) %reduce-scatter.20.cloned.1.call-update) | async-done | bytes 4194320 | tf_op jit(solution)/shard_map/reduce_scatter | solution.py:67
  (112 shorter events, 1.8 us)
Async XLA Ops:
  7.2 31.6 %copy-start.35 = (bf16[256,128]{1,0:T(8,128)(2,1)S(1)}, bf16[256,128]{1,0:T(8,128)(2,1)}, u32[]{:S(2)}) copy-start(bf16[256,128]{1,0:T(8,128)(2,1)} %param.14) | copy-start | bytes 196612
  7.2 46.0 %copy-start.34 = (bf16[256,128]{1,0:T(8,128)(2,1)S(1)}, bf16[256,128]{1,0:T(8,128)(2,1)}, u32[]{:S(2)}) copy-start(bf16[256,128]{1,0:T(8,128)(2,1)} %param.15) | copy-start | bytes 196612
  7.2 74.5 %all-gather.7.cloned.1.call-start = ((), (), s32[]{:S(2)}) async-start(), calls=%async_computation.7 | async-start | bytes 4718592 | tf_op jit(solution)/shard_map/all_gather | solution.py:55
  9.3 183.5 %all-gather.9.cloned.1.call-start = ((), (), s32[]{:S(2)}) async-start(), calls=%async_computation.8 | async-start | bytes 4718592 | tf_op jit(solution)/shard_map/all_gather | solution.py:59
  10.1 385.9 %all-gather.15.cloned.1.call-start = ((), (), s32[]{:S(2)}) async-start(), calls=%async_computation.11 | async-start | bytes 18874368 | tf_op jit(solution)/shard_map/all_gather | solution.py:59
  10.8 446.5 %all-gather.13.cloned.1.call-start = ((), (), s32[]{:S(2)}) async-start(), calls=%async_computation.10 | async-start | bytes 18874368 | tf_op jit(solution)/shard_map/all_gather | solution.py:55
  11.4 506.5 %all-gather.11.cloned.1.call-start = ((), (), s32[]{:S(2)}) async-start(), calls=%async_computation.9 | async-start | bytes 18874368 | tf_op jit(solution)/shard_map/all_gather | solution.py:55
  12.0 1459.8 %all-reduce.9.cloned.1.call-start = ((), (), s32[]{:S(2)}) async-start(), calls=%async_computation.19 | async-start | bytes 50331648 | tf_op jit(solution)/shard_map/psum | solution.py:95
  12.3 272.3 %copy-start.14 = (pred[1024,1024]{0,1:T(8,128)(4,1)}, pred[1024,1024]{0,1:T(8,128)(4,1)S(1)}, u32[]{:S(2)}) copy-start(pred[1024,1024]{0,1:T(8,128)(4,1)S(1)} %iota_compare_fusion) | copy-start | bytes 3145732
  23.1 49.5 %copy-start.22 = (f32[8,1,256]{2,1,0:T(1,128)}, f32[8,1,256]{2,1,0:T(1,128)S(1)}, u32[]{:S(2)}) copy-start(f32[8,1,256]{2,1,0:T(1,128)S(1)} %all-gather) | copy-start | bytes 24580
  29.4 52.3 %copy-start.16 = (f32[3,1024]{1,0:T(4,128)}, f32[3,1024]{1,0:T(4,128)S(1)}, u32[]{:S(2)}) copy-start(f32[3,1024]{1,0:T(4,128)S(1)} %broadcast_multiply_fusion) | copy-start | bytes 36868
  38.1 0.6 copy-start.25
  38.7 33.9 %copy-start.27 = (f32[3,1024]{1,0:T(4,128)}, f32[3,1024]{1,0:T(4,128)S(1)}, u32[]{:S(2)}) copy-start(f32[3,1024]{1,0:T(4,128)S(1)} %fusion.79) | copy-start | bytes 36868
  51.8 28.9 %copy-start.13 = (bf16[2048,128]{0,1:T(8,128)(2,1)}, bf16[2048,128]{0,1:T(8,128)(2,1)S(1)}, u32[]{:S(2)}) copy-start(bf16[2048,128]{0,1:T(8,128)(2,1)S(1)} %all_gather.33) | copy-start | bytes 1572868
  52.8 27.9 %copy-start.5 = (f32[1024,64]{0,1:T(8,128)}, f32[1024,64]{0,1:T(8,128)S(1)}, u32[]{:S(2)}) copy-start(f32[1024,64]{0,1:T(8,128)S(1)} %get-tuple-element.31) | copy-start | bytes 786436
  52.8 27.9 %copy-start.7 = (f32[1024,64]{0,1:T(8,128)}, f32[1024,64]{0,1:T(8,128)S(1)}, u32[]{:S(2)}) copy-start(f32[1024,64]{0,1:T(8,128)S(1)} %get-tuple-element.32) | copy-start | bytes 786436
  53.0 72.3 %copy-start.1 = (f32[1024,64]{1,0:T(8,128)}, f32[1024,64]{1,0:T(8,128)S(1)}, u32[]{:S(2)}) copy-start(f32[1024,64]{1,0:T(8,128)S(1)} %copy.81) | copy-start | bytes 786436
  53.2 72.0 %copy-start.3 = (f32[1024,64]{1,0:T(8,128)}, f32[1024,64]{1,0:T(8,128)S(1)}, u32[]{:S(2)}) copy-start(f32[1024,64]{1,0:T(8,128)S(1)} %copy.83) | copy-start | bytes 786436
  64.3 16.3 copy-start.12
  140.6 9.6 copy-start.21
  192.8 91.8 %copy-start.30 = (f32[3,1024,8]{1,2,0:T(8,128)}, f32[3,1024,8]{1,2,0:T(8,128)S(1)}, u32[]{:S(2)}) copy-start(f32[3,1024,8]{1,2,0:T(8,128)S(1)} %get-tuple-element.33) | copy-start | bytes 294916
  192.8 18.5 copy-start.19
  284.6 56.2 %copy-start.32 = (f32[3,1024,8]{1,2,0:T(8,128)}, f32[3,1024,8]{1,2,0:T(8,128)S(1)}, u32[]{:S(2)}) copy-start(f32[3,1024,8]{1,2,0:T(8,128)S(1)} %neg.20) | copy-start | bytes 294916
  284.6 56.2 %copy-start.2 = (f32[1024,64]{1,0:T(8,128)S(1)}, f32[1024,64]{1,0:T(8,128)}, u32[]{:S(2)}) copy-start(f32[1024,64]{1,0:T(8,128)} %copy-done.1) | copy-start | bytes 786436
  284.6 56.2 %copy-start.4 = (f32[1024,64]{1,0:T(8,128)S(1)}, f32[1024,64]{1,0:T(8,128)}, u32[]{:S(2)}) copy-start(f32[1024,64]{1,0:T(8,128)} %copy-done.3) | copy-start | bytes 786436
  357.2 18.3 copy-start.20
  395.9 61.3 %copy-start.17 = (f32[3,1024]{1,0:T(4,128)S(1)}, f32[3,1024]{1,0:T(4,128)}, u32[]{:S(2)}) copy-start(f32[3,1024]{1,0:T(4,128)} %copy-done.16) | copy-start | bytes 36868
  395.9 61.3 %copy-start.23 = (f32[8,1,256]{2,1,0:T(1,128)S(1)}, f32[8,1,256]{2,1,0:T(1,128)}, u32[]{:S(2)}) copy-start(f32[8,1,256]{2,1,0:T(1,128)} %copy-done.22) | copy-start | bytes 24580
  395.9 61.3 %copy-start.28 = (f32[3,1024]{1,0:T(4,128)S(1)}, f32[3,1024]{1,0:T(4,128)}, u32[]{:S(2)}) copy-start(f32[3,1024]{1,0:T(4,128)} %copy-done.27) | copy-start | bytes 36868
  849.8 26.8 %copy-start.15 = (pred[1024,1024]{0,1:T(8,128)(4,1)S(1)}, pred[1024,1024]{0,1:T(8,128)(4,1)}, u32[]{:S(2)}) copy-start(pred[1024,1024]{0,1:T(8,128)(4,1)} %copy-done.14) | copy-start | bytes 3145732
  849.8 26.8 %copy-start.31 = (f32[3,1024,8]{1,2,0:T(8,128)S(1)}, f32[3,1024,8]{1,2,0:T(8,128)}, u32[]{:S(2)}) copy-start(f32[3,1024,8]{1,2,0:T(8,128)} %copy-done.30) | copy-start | bytes 294916
  849.8 26.8 %copy-start.33 = (f32[3,1024,8]{1,2,0:T(8,128)S(1)}, f32[3,1024,8]{1,2,0:T(8,128)}, u32[]{:S(2)}) copy-start(f32[3,1024,8]{1,2,0:T(8,128)} %copy-done.32) | copy-start | bytes 294916
  849.8 704.2 %reduce-scatter.12.cloned.1.call-start = ((), (), s32[]{:S(2)}) async-start(), calls=%async_computation.14 | async-start | bytes 1179648 | tf_op jit(solution)/shard_map/reduce_scatter | solution.py:63
  876.6 201.2 %copy-start.6 = (f32[1024,64]{0,1:T(8,128)S(1)}, f32[1024,64]{0,1:T(8,128)}, u32[]{:S(2)}) copy-start(f32[1024,64]{0,1:T(8,128)} %copy-done.5) | copy-start | bytes 786436
  876.6 202.4 %copy-start.18 = (f32[3,1024]{1,0:T(4,128)S(1)}, f32[3,1024]{1,0:T(4,128)}, u32[]{:S(2)}) copy-start(f32[3,1024]{1,0:T(4,128)} %copy-done.16) | copy-start | bytes 36868
  876.6 202.4 %copy-start.24 = (f32[8,1,256]{2,1,0:T(1,128)S(1)}, f32[8,1,256]{2,1,0:T(1,128)}, u32[]{:S(2)}) copy-start(f32[8,1,256]{2,1,0:T(1,128)} %copy-done.22) | copy-start | bytes 24580
  876.6 202.4 %copy-start.29 = (f32[3,1024]{1,0:T(4,128)S(1)}, f32[3,1024]{1,0:T(4,128)}, u32[]{:S(2)}) copy-start(f32[3,1024]{1,0:T(4,128)} %copy-done.27) | copy-start | bytes 36868
  1079.0 21.8 copy-start.8
  1079.0 21.8 copy-start.10
  1090.8 463.2 %reduce-scatter.10.cloned.1.call-start = ((), (), s32[]{:S(2)}) async-start(), calls=%async_computation.13 | async-start | bytes 1179648 | tf_op jit(solution)/shard_map/reduce_scatter | solution.py:63
  1100.8 510.3 %reduce-scatter.14.cloned.1.call-start = ((), (), s32[]{:S(2)}) async-start(), calls=%async_computation.15 | async-start | bytes 9437184 | tf_op jit(solution)/shard_map/reduce_scatter | solution.py:67
  1119.7 561.1 %reduce-scatter.8.cloned.1.call-start = ((), (), s32[]{:S(2)}) async-start(), calls=%async_computation.12 | async-start | bytes 9437184 | tf_op jit(solution)/shard_map/reduce_scatter | solution.py:63
  1141.6 743.2 %reduce-scatter.16.cloned.1.call-start = ((), (), s32[]{:S(2)}) async-start(), calls=%async_computation.16 | async-start | bytes 37748736 | tf_op jit(solution)/shard_map/reduce_scatter | solution.py:63
  1210.2 878.5 %reduce-scatter.18.cloned.1.call-start = ((), (), s32[]{:S(2)}) async-start(), calls=%async_computation.17 | async-start | bytes 37748736 | tf_op jit(solution)/shard_map/reduce_scatter | solution.py:63
  1279.3 1013.2 %reduce-scatter.20.cloned.1.call-start = ((), (), s32[]{:S(2)}) async-start(), calls=%async_computation.18 | async-start | bytes 37748736 | tf_op jit(solution)/shard_map/reduce_scatter | solution.py:67
  1342.9 0.7 copy-start.36
  1342.9 1.9 copy-start.9
  1343.0 1.9 copy-start.11
  1343.0 128.8 %copy-start = (bf16[3,1024,256]{1,2,0:T(8,128)(2,1)S(1)}, bf16[3,1024,256]{1,2,0:T(8,128)(2,1)}, u32[]{:S(2)}) copy-start(bf16[3,1024,256]{1,2,0:T(8,128)(2,1)} %all-reduce.10) | copy-start | bytes 4718596
  1471.8 24.4 %copy-start.26 = (f32[3,1024]{1,0:T(4,128)S(1)}, f32[3,1024]{1,0:T(4,128)}, u32[]{:S(2)}) copy-start(f32[3,1024]{1,0:T(4,128)} %copy-done.25) | copy-start | bytes 36868
Sparse Core Ops, SparseCore 0:
  10.4 37.6 all-gather.6
  50.0 34.9 all-gather.8
  86.9 89.2 all-gather.14
  177.9 85.9 all-gather.12
  265.6 85.9 all-gather.10
  849.9 621.8 all-reduce.8
  1475.5 31.7 reduce-scatter.11
  1511.0 30.3 reduce-scatter.9
  1545.4 65.6 reduce-scatter.13
  1615.0 65.8 reduce-scatter.7
  1685.0 199.8 reduce-scatter.15
  1888.8 199.8 reduce-scatter.17
  2092.8 199.6 reduce-scatter.19
where the time goes:
time: 2310 us; the launch traced here: 2300 us
  matrix products  1080 us (47%)
  waiting for transfers between devices  857 us (37%)
  blocking collectives  195 us (8%)
  other arithmetic  116 us (5%)
  local copies, waits for them, and re-layouts  39.4 us (2%)
    dot_general x21, matrix products, matmul_f32(): return jnp.einsum(form, left, right, preferred_element_type=jnp.float32)  806 us
    reduce_scatter x5, waiting for transfers between devices, scatter_rows(): return lax.psum_scatter(grad_full, 'fsdp', scatter_dimension=0, tiled=True)  478 us
    reduce_scatter x2, waiting for transfers between devices, scatter_cols(): return lax.psum_scatter(grad_full, 'fsdp', scatter_dimension=1, tiled=True)  261 us
    psum x1, blocking collectives, device_step(): lax.psum(jnp.concatenate([dk_part, dv_part], axis=-1).astype(jnp.float32)...  146 us
    dot_general x3, matrix products, attend(): jnp.einsum('cril,cle->crie', att_prob, v_val, preferred_element_type=jnp....  120 us
    psum x1, waiting for transfers between devices, device_step(): branch_sum = lax.psum(branch_part, 'tp')  115 us
    dot_general x2, matrix products, attend(): jnp.einsum('crie,cle->cril', q_rot, k_rot, preferred_element_type=jnp.flo...  108 us
  transfers between devices with their start and end apart: 13, of which 6 were waited for; matrix products, arithmetic and copies ran while one was open for 39% of the time, Pallas kernels for 0%

commit v1 on v0

v1 whole, which is shorter than its diff:
```python
import math
import jax
import jax.numpy as jnp
from jax import lax
from jax.experimental import pallas as pl
from jax.experimental.pallas import tpu as pltpu
from jax.sharding import PartitionSpec as P

F32 = jnp.float32
BF16 = jnp.bfloat16
HEAD = 128
ROWS = 256


def dot_f32(left, right, left_dim, right_dim):
    return lax.dot_general(left, right, (((left_dim,), (right_dim,)), ((), ())), preferred_element_type=F32)


def prep_kernel(me_ref, x_ref, dy_ref, gain_ref, h_ref, h_own_ref, h_peer_ref, dy_own_ref, dy_peer_ref):
    x = x_ref[...].astype(F32)
    x_cent = x - jnp.mean(x, axis=-1, keepdims=True)
    x_var = jnp.mean(x_cent * x_cent, axis=-1, keepdims=True)
    h_ref[...] = (x_cent * lax.rsqrt(x_var + 1e-5) * gain_ref[...]).astype(BF16)
    me = me_ref[0]
    width = h_own_ref.shape[1] // 4
    for slot in range(4):
        own = pl.ds(pl.multiple_of((me ^ (2 * slot)) * width, width), width)
        peer = pl.ds(pl.multiple_of((me ^ (2 * slot + 1)) * width, width), width)
        here = slice(slot * width, (slot + 1) * width)
        h_own_ref[:, here] = h_ref[:, own]
        h_peer_ref[:, here] = h_ref[:, peer]
        dy_own_ref[:, here] = dy_ref[:, own]
        dy_peer_ref[:, here] = dy_ref[:, peer]


def prep(me, x2, dy2, gain):
    n_tok, width = x2.shape
    full = pl.BlockSpec((ROWS, width), lambda i, s: (i, 0))
    half = pl.BlockSpec((ROWS, width // 2), lambda i, s: (i, 0))
    return pl.pallas_call(
        prep_kernel,
        grid_spec=pltpu.PrefetchScalarGridSpec(
            num_scalar_prefetch=1,
            grid=(n_tok // ROWS,),
            in_specs=[full, full, pl.BlockSpec((1, width), lambda i, s: (0, 0))],
            out_specs=[full, half, half, half, half],
        ),
        out_shape=[jax.ShapeDtypeStruct((n_tok, width), BF16)] + [jax.ShapeDtypeStruct((n_tok, width // 2), BF16)] * 4,
        cost_estimate=pl.CostEstimate(flops=20 * n_tok * width, bytes_accessed=10 * n_tok * width, transcendentals=0),
        name="prep",
    )(me, x2, dy2, gain)


def turn(vals, cos_t, sin_t):
    return vals * cos_t + pltpu.roll(vals, HEAD // 2, 1) * sin_t


def att_kernel(q_ref, k_ref, v_ref, do_ref, cos_ref, sin_ref, o_ref, dq_ref, dkv_ref):
    seq_len = q_ref.shape[0]
    scale = 1.0 / math.sqrt(HEAD)
    k = turn(k_ref[...].astype(F32), cos_ref[...], sin_ref[...]).astype(BF16)
    v = v_ref[...]

    @pl.when(pl.program_id(1) == 0)
    def _():
        dkv_ref[...] = jnp.zeros_like(dkv_ref)

    block = 256
    for i in range(seq_len // block):
        here = slice(i * block, (i + 1) * block)
        seen = (i + 1) * block
        cos_t = cos_ref[here, :]
        sin_t = sin_ref[here, :]
        q = (turn(q_ref[here, :].astype(F32), cos_t, sin_t) * scale).astype(BF16)
        d_out = do_ref[here, :]
        scores = dot_f32(q, k[:seen], 1, 1)
        row = lax.broadcasted_iota(jnp.int32, (block, seen), 0) + i * block
        col = lax.broadcasted_iota(jnp.int32, (block, seen), 1)
        scores = jnp.where(row >= col, scores, -1e30)
        exp_val = jnp.exp(scores - jnp.max(scores, axis=-1, keepdims=True))
        prob = exp_val * (1.0 / jnp.sum(exp_val, axis=-1, keepdims=True))
        prob_b = prob.astype(BF16)
        o_ref[here, :] = dot_f32(prob_b, v[:seen], 1, 0).astype(BF16)
        d_prob = dot_f32(d_out, v[:seen], 1, 1).astype(BF16).astype(F32)
        d_row = jnp.sum(d_prob * prob, axis=-1, keepdims=True)
        d_scores = (prob * (d_prob - d_row)).astype(BF16)
        d_q = dot_f32(d_scores, k[:seen], 1, 0).astype(BF16).astype(F32) * scale
        dq_ref[here, :] = turn(d_q, cos_t, -sin_t).astype(BF16)
        dkv_ref[:seen, :HEAD] += dot_f32(d_scores, q, 0, 0)
        dkv_ref[:seen, HEAD:] += dot_f32(prob_b, d_out, 0, 0)


def attention(qkv, d_att, cos_t, sin_t, seq_len):
    n_tok, inner = d_att.shape
    n_heads = inner // HEAD
    n_batch = n_tok // seq_len
    head = pl.BlockSpec((seq_len, HEAD), lambda b, h: (b, h))
    table = pl.BlockSpec((seq_len, HEAD), lambda b, h: (0, 0))
    flops = 12 * n_batch * n_heads * seq_len * seq_len * HEAD
    return pl.pallas_call(
        att_kernel,
        grid=(n_batch, n_heads),
        in_specs=[
            head,
            pl.BlockSpec((seq_len, HEAD), lambda b, h: (b, n_heads)),
            pl.BlockSpec((seq_len, HEAD), lambda b, h: (b, n_heads + 1)),
            head,
            table,
            table,
        ],
        out_specs=[head, head, pl.BlockSpec((seq_len, 2 * HEAD), lambda b, h: (b, 0))],
        out_shape=[
            jax.ShapeDtypeStruct((n_tok, inner), BF16),
            jax.ShapeDtypeStruct(qkv.shape, BF16),
            jax.ShapeDtypeStruct((n_tok, 2 * HEAD), F32),
        ],
        cost_estimate=pl.CostEstimate(flops=flops, bytes_accessed=8 * n_tok * inner, transcendentals=n_batch * n_heads * seq_len * seq_len),
        name="attention",
    )(qkv, qkv, qkv, d_att, cos_t, sin_t)


def kv_kernel(own_ref, peer_ref, cos_ref, sin_ref, held_ref, out_ref):
    total = (own_ref[...] + peer_ref[...]).astype(BF16)
    d_k = total[:, :HEAD].astype(F32)
    out_ref[:, :HEAD] = turn(d_k, cos_ref[...], -sin_ref[...]).astype(BF16)
    out_ref[:, HEAD:] = total[:, HEAD:]


def kv_finish(own, peer, cos_t, sin_t, d_qkv):
    n_tok = own.shape[0]
    per_seq = cos_t.shape[0] // ROWS
    part = pl.BlockSpec((ROWS, 2 * HEAD), lambda i: (i, 0))
    table = pl.BlockSpec((ROWS, HEAD), lambda i: (i % per_seq, 0))
    last = d_qkv.shape[1] // (2 * HEAD) - 1
    return pl.pallas_call(
        kv_kernel,
        grid=(n_tok // ROWS,),
        in_specs=[part, part, table, table, pl.BlockSpec(memory_space=pl.ANY)],
        out_specs=pl.BlockSpec((ROWS, 2 * HEAD), lambda i: (i, last)),
        out_shape=jax.ShapeDtypeStruct(d_qkv.shape, BF16),
        input_output_aliases={4: 0},
        cost_estimate=pl.CostEstimate(flops=20 * own.size, bytes_accessed=10 * own.size, transcendentals=0),
        name="kv_finish",
    )(own, peer, cos_t, sin_t, d_qkv)


def y_kernel(x_ref, own_ref, peer_ref, *refs):
    branch = own_ref[...].astype(F32) + peer_ref[...].astype(F32)
    refs[-1][...] = (x_ref[...].astype(F32) + branch).astype(BF16)


def y_finish(index, x2, own, peer, held):
    rows, width = own.shape
    steps = rows // ROWS
    whole = pl.BlockSpec((ROWS, width), lambda i: (index * steps + i, 0))
    part = pl.BlockSpec((ROWS, width), lambda i: (i, 0))
    extra = [] if held is None else [held]
    return pl.pallas_call(
        y_kernel,
        grid=(steps,),
        in_specs=[whole, part, part] + [pl.BlockSpec(memory_space=pl.ANY)] * len(extra),
        out_specs=whole,
        out_shape=jax.ShapeDtypeStruct(x2.shape, BF16),
        input_output_aliases={3: 0} if extra else {},
        cost_estimate=pl.CostEstimate(flops=20 * own.size, bytes_accessed=8 * own.size, transcendentals=0),
        name="y_finish",
    )(x2, own, peer, *extra)


def norm_kernel(x_ref, dy_ref, own_ref, peer_ref, gain_ref, *refs):
    grad_ref, part_ref = refs[-2:]

    @pl.when(pl.program_id(0) == 0)
    def _():
        part_ref[...] = jnp.zeros_like(part_ref)

    x = x_ref[...].astype(F32)
    x_cent = x - jnp.mean(x, axis=-1, keepdims=True)
    rstd = lax.rsqrt(jnp.mean(x_cent * x_cent, axis=-1, keepdims=True) + 1e-5)
    x_hat = x_cent * rstd
    d_h = (own_ref[...].astype(F32) + peer_ref[...].astype(F32)).astype(BF16).astype(F32)
    part_ref[...] += jnp.sum(d_h * x_hat, axis=0, keepdims=True)
    d_hat = d_h * gain_ref[...]
    mean_d = jnp.mean(d_hat, axis=-1, keepdims=True)
    mean_dx = jnp.mean(d_hat * x_hat, axis=-1, keepdims=True)
    d_x = rstd * (d_hat - mean_d - x_hat * mean_dx)
    grad_ref[...] = (dy_ref[...].astype(F32) + d_x).astype(BF16)


def norm_finish(index, x2, dy2, own, peer, gain, held):
    rows, width = own.shape
    steps = rows // ROWS
    whole = pl.BlockSpec((ROWS, width), lambda i: (index * steps + i, 0))
    part = pl.BlockSpec((ROWS, width), lambda i: (i, 0))
    line = pl.BlockSpec((1, width), lambda i: (0, 0))
    extra = [] if held is None else [held]
    return pl.pallas_call(
        norm_kernel,
        grid=(steps,),
        in_specs=[whole, whole, part, part, line] + [pl.BlockSpec(memory_space=pl.ANY)] * len(extra),
        out_specs=[whole, line],
        out_shape=[jax.ShapeDtypeStruct(x2.shape, BF16), jax.ShapeDtypeStruct((1, width), F32)],
        input_output_aliases={5: 0} if extra else {},
        cost_estimate=pl.CostEstimate(flops=50 * own.size, bytes_accessed=10 * own.size, transcendentals=0),
        name="norm_finish",
    )(x2, dy2, own, peer, gain, *extra)


def swiglu(gate_val, up_val):
    return (jax.nn.silu(gate_val.astype(F32)) * up_val.astype(F32)).astype(BF16)


def swap(vals, bit, n_dev):
    return lax.ppermute(vals, 'fsdp', [(i, i ^ bit) for i in range(n_dev)])


def after(vals, *others):
    return lax.optimization_barrier((vals,) + others)[0]


class BlockSum:
    def __init__(self, to_peer, axis, n_dev):
        self.axis = axis
        self.n_dev = n_dev
        self.to_peer = to_peer.astype(BF16)
        self.from_peer = swap(self.to_peer, 1, n_dev)

    def cut(self, slot, half, vals=None):
        vals = self.own if vals is None else vals
        width = self.own.shape[self.axis] // 4
        middle = self.own.shape[1 - self.axis] // 2
        index = [None, None]
        index[self.axis] = slice(slot * width, (slot + 1) * width)
        index[1 - self.axis] = slice(half * middle, (half + 1) * middle)
        return vals[tuple(index)]

    plan = ((0, 2, 4, 1, 2), (1, 4, 2, 2, 1))

    def first(self, left, right):
        self.own = dot_f32(left, right, 0, 0) + self.from_peer.astype(F32)
        rounded = self.own.astype(BF16)
        self.came = []
        for half, first_bit, _, first_slot, _ in self.plan:
            sent = jnp.concatenate([self.cut(first_slot, half, rounded), self.cut(3, half, rounded)], axis=self.axis)
            self.came.append(swap(sent, first_bit, self.n_dev))
        return self.own

    def second(self):
        self.last = []
        self.near = []
        self.sent = []
        for came, (half, _, second_bit, _, second_slot) in zip(self.came, self.plan):
            near, far = jnp.split(came, 2, axis=self.axis)
            sent = (self.cut(second_slot, half) + far.astype(F32)).astype(BF16)
            self.sent.append(sent)
            self.near.append(near)
            self.last.append(swap(sent, second_bit, self.n_dev))
        return self.sent

    def total(self):
        self.last = lax.optimization_barrier(self.last)
        sums = []
        for half in range(2):
            sums.append(self.cut(0, half) + self.near[half].astype(F32) + self.last[half].astype(F32))
        return jnp.concatenate(sums, axis=1 - self.axis)


def solution(mesh):
    n_dev = mesh.shape['fsdp']

    def device_step(x_in, dy_out, ln_gain, w_q, w_k, w_v, w_o, w_gate, w_up, w_down):
        n_batch, seq_len, width = x_in.shape
        n_tok = n_batch * seq_len
        inner = w_q.shape[1]
        x2 = x_in.reshape(n_tok, width)
        dy2 = dy_out.reshape(n_tok, width)
        me = lax.axis_index('fsdp').astype(jnp.int32).reshape(1)

        def tp_peer(vals):
            return lax.ppermute(vals, 'tp', [(0, 1), (1, 0)])

        gain = lax.all_gather(ln_gain, 'fsdp', tiled=True).reshape(1, width)
        w_qkv = lax.all_gather(jnp.concatenate([w_q, w_k, w_v], axis=1), 'fsdp', axis=0, tiled=True)
        wo = lax.all_gather(w_o, 'fsdp', axis=1, tiled=True)
        wg = lax.all_gather(w_gate, 'fsdp', axis=0, tiled=True)
        wu = lax.all_gather(w_up, 'fsdp', axis=0, tiled=True)
        wd = lax.all_gather(w_down, 'fsdp', axis=1, tiled=True)

        half_dim = HEAD // 2
        inv_freq = jnp.power(10000.0, -2.0 * jnp.arange(half_dim, dtype=F32) / HEAD)
        angle = jnp.arange(seq_len, dtype=F32)[:, None] * inv_freq[None, :]
        cos_t = jnp.concatenate([jnp.cos(angle), jnp.cos(angle)], axis=1)
        sin_t = jnp.concatenate([-jnp.sin(angle), jnp.sin(angle)], axis=1)

        h_norm, h_own, h_peer, dy_own, dy_peer = prep(me, x2, dy2, gain)

        qkv = dot_f32(h_norm, w_qkv, 1, 0).astype(BF16)
        d_att = dot_f32(dy2, wo, 1, 1).astype(BF16)
        att, d_q, dkv = attention(qkv, d_att, cos_t, sin_t, seq_len)
        d_qkv = kv_finish(dkv, tp_peer(dkv), cos_t, sin_t, d_q)

        gate_val = dot_f32(h_norm, wg, 1, 0).astype(BF16)
        up_val = dot_f32(h_norm, wu, 1, 0).astype(BF16)
        act = swiglu(gate_val, up_val)

        def rows_of(vals, b):
            return vals[b * seq_len:(b + 1) * seq_len]

        def y_part(b, act_b):
            part = dot_f32(rows_of(att, b), wo, 1, 0) + dot_f32(rows_of(act_b, b), wd, 1, 0)
            part = part.astype(BF16)
            return part, tp_peer(part)

        column = lax.broadcasted_iota(jnp.int32, (1, inner + 2 * HEAD), 1)
        is_k = (column >= inner) & (column < inner + HEAD)
        is_v = column >= inner + HEAD
        skip = jnp.where(lax.axis_index('tp') == 0, is_v, is_k)
        w_back = jnp.where(skip, jnp.zeros((), BF16), w_qkv)

        def h_part(b, d_gate_b, d_up_b):
            part = dot_f32(rows_of(d_qkv, b), w_back, 1, 1) + dot_f32(rows_of(d_gate_b, b), wg, 1, 1)
            part = (part + dot_f32(rows_of(d_up_b, b), wu, 1, 1)).astype(BF16)
            return part, tp_peer(part)

        y0, y0_peer = y_part(0, act)
        y1, y1_peer = y_part(1, after(act, y0))
        down = BlockSum(dot_f32(after(act, y1), dy_peer, 0, 0), 1, n_dev)
        y2, y2_peer = y_part(2, after(act, down.to_peer))
        down_own = down.first(after(act, y2), dy_own)

        d_act = dot_f32(after(dy2, down_own), wd, 1, 1).astype(BF16)
        _, act_pull = jax.vjp(swiglu, gate_val, up_val)
        d_gate, d_up = act_pull(d_act)

        h0, h0_peer = h_part(0, d_gate, d_up)
        down_sent = down.second()
        gate = BlockSum(dot_f32(h_peer, after(d_gate, h0, *down_sent), 0, 0), 0, n_dev)
        h1, h1_peer = h_part(1, after(d_gate, gate.to_peer), d_up)
        gate_own = gate.first(h_own, after(d_gate, h1))
        y_out = y_finish(0, x2, after(y0, gate_own), y0_peer, None)
        y_out = y_finish(1, x2, after(y1, gate_own), y1_peer, y_out)
        up = BlockSum(dot_f32(h_peer, after(d_up, gate_own, y_out), 0, 0), 0, n_dev)
        h2, h2_peer = h_part(2, d_gate, after(d_up, up.to_peer))
        gate_sent = gate.second()
        up_own = up.first(h_own, after(d_up, h2, *gate_sent))
        grad_wdown = down.total()
        y_out = y_finish(2, x2, after(y2, up_own), y2_peer, y_out)

        att_late = after(att, up_own)
        small_o = BlockSum(dot_f32(att_late, dy_peer, 0, 0), 1, n_dev)
        d_late = after(d_qkv, small_o.to_peer)
        small_q = BlockSum(dot_f32(h_peer, d_late, 0, 0), 0, n_dev)
        o_own = small_o.first(after(att_late, small_q.to_peer), dy_own)
        q_own = small_q.first(h_own, after(d_late, o_own))
        grad_wgate = gate.total()
        up_sent = up.second()
        grad_x, gain_part = norm_finish(0, x2, dy2, after(h0, q_own, *up_sent), h0_peer, gain, None)
        o_sent = small_o.second()
        q_sent = small_q.second()
        grad_x, gain_b = norm_finish(1, x2, dy2, after(h1, q_own, *up_sent), h1_peer, gain, grad_x)
        gain_part = gain_part + gain_b
        grad_wup = up.total()
        grad_wo = small_o.total()
        grad_qkv = small_q.total()
        grad_x, gain_b = norm_finish(2, x2, dy2, after(h2, *o_sent, *q_sent), h2_peer, gain, grad_x)
        gain_part = gain_part + gain_b
        grad_gain = lax.psum_scatter(gain_part.reshape(width), 'fsdp', scatter_dimension=0, tiled=True)

        shape = (n_batch, seq_len, width)
        return (y_out.reshape(shape), grad_x.reshape(shape), grad_gain, grad_qkv[:, :inner], grad_qkv[:, inner:inner + HEAD], grad_qkv[:, inner + HEAD:], grad_wo, grad_wgate, grad_wup, grad_wdown)

    act_spec = P('fsdp', None, None)
    row_spec = P('fsdp', 'tp')
    kv_spec = P('fsdp', None)
    col_spec = P('tp', 'fsdp')
    in_specs = (act_spec, act_spec, P('fsdp'), row_spec, kv_spec, kv_spec, col_spec, row_spec, row_spec, col_spec)
    out_specs = (act_spec, act_spec, P('fsdp'), row_spec, kv_spec, kv_spec, col_spec, row_spec, row_spec, col_spec)

    return jax.shard_map(device_step, mesh=mesh, in_specs=in_specs, out_specs=out_specs, check_vma=False)
```

time: 2310 us -> 1430 us (0.62)
  waiting for transfers between devices: 857 us -> 292 us
  matrix products: 1080 us -> 794 us
  Pallas kernels: 0 us -> 209 us
  blocking collectives: 195 us -> 23.3 us
  other arithmetic: 116 us -> 49.1 us
  starting transfers between devices: 0.52 us -> 29.4 us
  local copies, waits for them, and re-layouts: 39.4 us -> 11.7 us
    reduce_scatter x7 -> x0, waiting for transfers between devices: 739 us -> none  [the longest x5 478 us: scatter_rows(): return lax.psum_scatter(grad_full, 'fsdp', scatter_dimension=0, tiled=True)]
    ppermute x0 -> x32, waiting for transfers between devices: none -> 274 us  [the longest x7 222 us: tp_peer(): return lax.ppermute(vals, 'tp', [(0, 1), (1, 0)])]
    dot_general x26 -> x30, matrix products: 1030 us -> 794 us  [dot_f32(): lax.dot_general(left, right, (((left_dim,), (right_dim,)), ((), ())), pre...]
    pallas_call x0 -> x9, Pallas kernels: none -> 209 us  [the longest x1 116 us: attention(): pl.pallas_call(att_kernel, grid=(n_batch, n_heads), in_specs=[head, pl.Bl...]
    psum x1 -> x0, blocking collectives: 146 us -> none  [device_step(): lax.psum(jnp.concatenate([dk_part, dv_part], axis=-1).astype(jnp.float32)...]
    psum x1 -> x0, waiting for transfers between devices: 115 us -> none  [device_step(): branch_sum = lax.psum(branch_part, 'tp')]
    sub x1 -> x0, matrix products: 42.6 us -> none  [attend(): exp_val = jnp.exp(scores - row_max)]
    convert_element_type x5, other arithmetic: 50.6 us -> 14.7 us  [second(): sent = (self.cut(second_slot, half) + far.astype(F32)).astype(BF16)]
  transfers between devices with their start and end apart: 13 -> 37, of which waited for: 6 -> 13; matrix products, arithmetic and copies ran while one was open for 39% -> 54% of each run, Pallas kernels for 0% -> 15%
where the time goes in v1:
time: 1430 us; the launch traced here: 1420 us
  matrix products  794 us (56%)
  waiting for transfers between devices  292 us (20%)
  Pallas kernels  209 us (15%)
  other arithmetic  49.1 us (3%)
  starting transfers between devices  29.4 us (2%)
  blocking collectives  23.3 us (2%)
  between operations  15.1 us (1%)
    dot_general x30, matrix products, dot_f32(): lax.dot_general(left, right, (((left_dim,), (right_dim,)), ((), ())), pre...  794 us
    ppermute x7, waiting for transfers between devices, tp_peer(): return lax.ppermute(vals, 'tp', [(0, 1), (1, 0)])  222 us
    pallas_call x1, Pallas kernels, attention(): pl.pallas_call(att_kernel, grid=(n_batch, n_heads), in_specs=[head, pl.Bl...  116 us
    ppermute x25, waiting for transfers between devices, swap(): return lax.ppermute(vals, 'fsdp', [(i, i ^ bit) for i in range(n_dev)])  51.9 us
    pallas_call x3, Pallas kernels, norm_finish(): pl.pallas_call(norm_kernel, grid=(steps,), in_specs=[whole, whole, part,...  37 us
  transfers between devices with their start and end apart: 37, of which 13 were waited for; matrix products, arithmetic and copies ran while one was open for 54% of the time, Pallas kernels for 15%

profile of v1, /device:TPU:0, one launch (start us, length us, event | category | flops | bytes accessed | tf_op | source)
XLA Modules:
  0.0 1423.2 jit_solution(18402186053062197791)
XLA Ops:
  8.0 2.0 pad_maximum_fusion.8
  11.9 10.8 all-gather
  22.7 2.0 fusion.69
  26.0 25.6 %prep.1 = (bf16[3072,2048]{1,0:T(8,128)(2,1)}, bf16[3072,1024]{1,0:T(8,128)(2,1)}, bf16[3072,1024]{1,0:T(8,128)(2,1)}, bf16[3072,1024]{1,0:T(8,128)(2,1)}, bf16[3072,1024]{1,0:T(8,128)(2,1)}) custom-call(s32[1]{0:T(128)} %bitcast.1.me_ref, bf16[3072,2048]{1,0:T(8,128)(2,1)} %bitcast.51, bf16[3072,2048]{1,0:T(8,128)(2,1)} %bitcast.58, f32[1,2048]{1,0:T(1,128)} %bitcast.70), custom_call_target="tpu_custom_call" | custom-call | flops 125829120 | bytes 62914560 | tf_op jit(solution)/shard_map/prep/pallas_call | solution.py:40
  51.6 18.9 %convolution_convert_fusion.7.do_ref = bf16[3072,1024]{1,0:T(8,128)(2,1)} fusion(bf16[3072,2048]{1,0:T(8,128)(2,1)} %bitcast.59, bf16[1024,2048]{1,0:T(8,128)(2,1)} %all-gather.9.cloned.1.call-done), kind=kOutput, calls=%fused_computation.49 | convolution fusion | flops 12888047616 | bytes 23068672 | tf_op jit(solution)/shard_map/dot_general | solution.py:16
  70.4 15.5 %all-gather.7.cloned.1.call-done = bf16[2048,1280]{1,0:T(8,128)(2,1)} async-done(((bf16[256,1280]{1,0:T(8,128)(2,1)}), bf16[2048,1280]{1,0:T(8,128)(2,1)}) %all-gather.7.cloned.1.call-update) | async-done | bytes 5242896 | tf_op jit(solution)/shard_map/all_gather | solution.py:283
  86.0 22.0 %convolution_convert_fusion.3.q_ref.k_ref.v_ref = bf16[3072,1280]{1,0:T(8,128)(2,1)} fusion(bf16[3072,2048]{1,0:T(8,128)(2,1)} %get-tuple-element.55, bf16[2048,1280]{1,0:T(8,128)(2,1)} %all-gather.7.cloned.1.call-done), kind=kOutput, calls=%fused_computation.21 | convolution fusion | flops 16110059520 | bytes 25690112 | tf_op jit(solution)/shard_map/dot_general | solution.py:16
  107.9 115.5 %attention.1 = (bf16[3072,1024]{1,0:T(8,128)(2,1)}, bf16[3072,1280]{1,0:T(8,128)(2,1)}, f32[3072,256]{1,0:T(8,128)}) custom-call(bf16[3072,1280]{1,0:T(8,128)(2,1)} %convolution_convert_fusion.3.q_ref.k_ref.v_ref, bf16[3072,1280]{1,0:T(8,128)(2,1)} %convolution_convert_fusion.3.q_ref.k_ref.v_ref, ...), custom_call_target="tpu_custom_call" | custom-call | flops 38654705664 | bytes 25165824 | tf_op jit(solution)/shard_map/attention/pallas_call | solution.py:100
  223.5 10.7 fusion.53
  234.2 8.3 fusion.55
  242.4 60.9 %convolution_convert_fusion.2 = bf16[3072,4096]{1,0:T(8,128)(2,1)} fusion(bf16[3072,2048]{1,0:T(8,128)(2,1)} %get-tuple-element.55, bf16[2048,4096]{1,0:T(8,128)(2,1)} %all-gather.11.cloned.1.call-done), kind=kOutput, calls=%fused_computation.17 | convolution fusion | flops 51552190464 | bytes 54525952 | tf_op jit(solution)/shard_map/dot_general | solution.py:16
  303.3 70.1 %fusion = (bf16[3072,4096]{1,0:T(8,128)(2,1)}, bf16[3072,4096]{1,0:T(8,128)(2,1)}) fusion(bf16[3072,4096]{1,0:T(8,128)(2,1)} %convolution_convert_fusion.2, bf16[3072,2048]{1,0:T(8,128)(2,1)} %get-tuple-element.55, bf16[2048,4096]{1,0:T(8,128)(2,1)} %all-gather.13.cloned.1.call-done), kind=kOutput, calls=%fused_computation.7 | convolution fusion | flops 51652853760 | bytes 104857600 | tf_op jit(solution)/shard_map/dot_general | solution.py:16
  373.4 24.4 %add_convert_fusion.5.own_ref = bf16[1024,2048]{1,0:T(8,128)(2,1)} fusion(f32[1024,2048]{1,0:T(8,128)} %fusion.53, bf16[4096,2048]{1,0:T(8,128)(2,1)} %all-gather.15.cloned.1.call-done, bf16[3072,4096]{1,0:T(8,128)(2,1)} %get-tuple-element.62), kind=kOutput, calls=%fused_computation.45 | convolution fusion | flops 17184063488 | bytes 37748736 | tf_op jit(solution)/shard_map/dot_general | solution.py:16
  397.8 22.6 %add_convert_fusion.4.own_ref = bf16[1024,2048]{1,0:T(8,128)(2,1)} fusion(f32[1024,2048]{1,0:T(8,128)} %fusion.55, bf16[4096,2048]{1,0:T(8,128)(2,1)S(1)} %copy-done.16, bf16[3072,4096]{1,0:T(8,128)(2,1)} %get-tuple-element.62), kind=kOutput, calls=%fused_computation.42 | convolution fusion | flops 17184063488 | bytes 37748736 | tf_op jit(solution)/shard_map/dot_general | solution.py:16
  420.4 33.5 %convolution_convert_fusion.6 = bf16[4096,1024]{1,0:T(8,128)(2,1)} fusion(bf16[3072,4096]{1,0:T(8,128)(2,1)} %get-tuple-element.62, bf16[3072,1024]{1,0:T(8,128)(2,1)} %get-tuple-element.59), kind=kOutput, calls=%fused_computation.48 | convolution fusion | flops 25773998080 | bytes 39845888 | tf_op jit(solution)/shard_map/dot_general | solution.py:16
  457.6 10.7 fusion.57
  468.3 56.2 %collective-permute-done.1.peer_ref = f32[3072,256]{1,0:T(8,128)} collective-permute-done((f32[3072,256]{1,0:T(8,128)S(1)}, f32[3072,256]{1,0:T(8,128)}, u32[]{:S(2)}, u32[]{:S(2)}) %collective-permute-start.1) | collective-permute-done | bytes 3145760 | tf_op jit(solution)/shard_map/ppermute | solution.py:280
  524.5 9.2 kv_finish.1
  535.8 24.3 %add_convert_fusion.3.own_ref = bf16[1024,2048]{1,0:T(8,128)(2,1)} fusion(f32[1024,2048]{1,0:T(8,128)} %fusion.57, bf16[4096,2048]{1,0:T(8,128)(2,1)} %all-gather.15.cloned.1.call-done, bf16[3072,4096]{1,0:T(8,128)(2,1)} %get-tuple-element.62), kind=kOutput, calls=%fused_computation.39 | convolution fusion | flops 17184063488 | bytes 37748736 | tf_op jit(solution)/shard_map/dot_general | solution.py:16
  560.1 32.7 %fusion.79 = (bf16[4096,1024]{1,0:T(8,128)(2,1)S(1)}, f32[4096,1024]{1,0:T(8,128)}) fusion(bf16[4096,1024]{1,0:T(8,128)(2,1)} %collective-permute-done, bf16[3072,4096]{1,0:T(8,128)(2,1)} %get-tuple-element.62, bf16[3072,1024]{1,0:T(8,128)(2,1)S(1)} %bitcast.79), kind=kOutput, calls=%fused_computation.141 | convolution fusion | flops 25782386688 | bytes 65011712 | tf_op jit(solution)/shard_map/dot_general | solution.py:16
  598.2 86.7 %fusion.7 = (bf16[3072,4096]{1,0:T(8,128)(2,1)}, bf16[3072,4096]{1,0:T(8,128)(2,1)}) fusion(bf16[3072,4096]{1,0:T(8,128)(2,1)} %convolution_convert_fusion.2, bf16[3072,4096]{1,0:T(8,128)(2,1)} %get-tuple-element.148, bf16[3072,2048]{1,0:T(8,128)(2,1)} %bitcast.60, bf16[4096,2048]{1,0:T(8,128)(2,1)} %all-gather.15.cloned.1.call-done), kind=kOutput, calls=%fused_computation.14 | convolution fusion | flops 51766099968 | bytes 130023424 | tf_op jit(solution)/shard_map/dot_general | solution.py:16
  684.9 24.8 %fusion.10 = f32[1024,2048]{1,0:T(8,128)} fusion(bf16[2048,4096]{1,0:T(8,128)(2,1)} %all-gather.13.cloned.1.call-done, bf16[3072,4096]{1,0:T(8,128)(2,1)} %get-tuple-element.75), kind=kOutput, calls=%fused_computation.24 | convolution fusion | flops 17179869184 | bytes 33554432 | tf_op jit(solution)/shard_map/dot_general | solution.py:16
  709.7 24.2 %fusion.8 = f32[1024,2048]{1,0:T(8,128)} fusion(bf16[2048,4096]{1,0:T(8,128)(2,1)} %all-gather.13.cloned.1.call-done, bf16[3072,4096]{1,0:T(8,128)(2,1)} %get-tuple-element.75), kind=kOutput, calls=%fused_computation.22 | convolution fusion | flops 17179869184 | bytes 33554432 | tf_op jit(solution)/shard_map/dot_general | solution.py:16
  733.9 24.3 %fusion.12 = f32[1024,2048]{1,0:T(8,128)} fusion(bf16[2048,4096]{1,0:T(8,128)(2,1)} %all-gather.11.cloned.1.call-done, bf16[3072,4096]{1,0:T(8,128)(2,1)} %get-tuple-element.70), kind=kOutput, calls=%fused_computation.26 | convolution fusion | flops 17179869184 | bytes 33554432 | tf_op jit(solution)/shard_map/dot_general | solution.py:16
  758.3 12.5 add_convert_fusion.2.own_ref
  770.8 3.3 fusion.51
  774.1 33.2 %convolution_convert_fusion.5 = bf16[1024,4096]{1,0:T(8,128)(2,1)} fusion(bf16[3072,1024]{1,0:T(8,128)(2,1)} %get-tuple-element.67, bf16[3072,4096]{1,0:T(8,128)(2,1)} %get-tuple-element.70), kind=kOutput, calls=%fused_computation.47 | convolution fusion | flops 25773998080 | bytes 39845888 | tf_op jit(solution)/shard_map/dot_general | solution.py:16
  807.4 24.4 %fusion.14 = f32[1024,2048]{1,0:T(8,128)} fusion(bf16[2048,4096]{1,0:T(8,128)(2,1)} %all-gather.11.cloned.1.call-done, bf16[3072,4096]{1,0:T(8,128)(2,1)} %get-tuple-element.70), kind=kOutput, calls=%fused_computation.28 | convolution fusion | flops 17179869184 | bytes 33554432 | tf_op jit(solution)/shard_map/dot_general | solution.py:16
  833.7 24.1 %fusion.20 = f32[1024,2048]{1,0:T(8,128)} fusion(bf16[2048,4096]{1,0:T(8,128)(2,1)} %all-gather.11.cloned.1.call-done, bf16[3072,4096]{1,0:T(8,128)(2,1)} %get-tuple-element.70), kind=kOutput, calls=%fused_computation.36 | convolution fusion | flops 17179869184 | bytes 33554432 | tf_op jit(solution)/shard_map/dot_general | solution.py:16
  857.8 12.3 add_convert_fusion.1.own_ref
  871.6 5.0 fusion.42
  876.6 35.4 %fusion.78 = (bf16[1024,4096]{1,0:T(8,128)(2,1)}, f32[1024,4096]{1,0:T(8,128)}) fusion(bf16[1024,4096]{1,0:T(8,128)(2,1)} %collective-permute-done.4, bf16[3072,1024]{1,0:T(8,128)(2,1)} %get-tuple-element.61, bf16[3072,4096]{1,0:T(8,128)(2,1)} %get-tuple-element.70), kind=kOutput, calls=%fused_computation.140 | convolution fusion | flops 25782386688 | bytes 65011712 | tf_op jit(solution)/shard_map/dot_general | solution.py:16
  912.1 7.2 y_finish.3.refs_0_
  919.3 7.2 y_finish.4.refs_0_
  926.5 33.6 %convolution_convert_fusion.4 = bf16[1024,4096]{1,0:T(8,128)(2,1)} fusion(bf16[3072,1024]{1,0:T(8,128)(2,1)} %get-tuple-element.67, bf16[3072,4096]{1,0:T(8,128)(2,1)} %get-tuple-element.75), kind=kOutput, calls=%fused_computation.46 | convolution fusion | flops 25773998080 | bytes 39845888 | tf_op jit(solution)/shard_map/dot_general | solution.py:16
  960.1 2.3 pad_maximum_fusion.2
  962.4 1.7 concatenate.73
  964.1 1.9 fusion.81
  968.4 24.3 %fusion.18 = f32[1024,2048]{1,0:T(8,128)} fusion(bf16[2048,4096]{1,0:T(8,128)(2,1)} %all-gather.13.cloned.1.call-done, bf16[3072,4096]{1,0:T(8,128)(2,1)} %get-tuple-element.75), kind=kOutput, calls=%fused_computation.33 | convolution fusion | flops 17179869184 | bytes 33554432 | tf_op jit(solution)/shard_map/dot_general | solution.py:16
  992.7 21.7 %collective-permute-done.7 = bf16[512,2048]{1,0:T(8,128)(2,1)S(1)} collective-permute-done((bf16[512,2048]{1,0:T(8,128)(2,1)S(1)}, bf16[512,2048]{1,0:T(8,128)(2,1)S(1)}, u32[]{:S(2)}, u32[]{:S(2)}) %collective-permute-start.7) | collective-permute-done | bytes 2097184 | tf_op jit(solution)/shard_map/ppermute | solution.py:214
  1016.9 4.3 fusion.49
  1023.1 12.5 add_convert_fusion.own_ref
  1035.6 10.2 collective-permute-done.26
  1046.2 3.7 fusion.46
  1050.0 35.0 %fusion.75 = (bf16[1024,4096]{1,0:T(8,128)(2,1)}, f32[1024,4096]{1,0:T(8,128)}) fusion(bf16[1024,4096]{1,0:T(8,128)(2,1)} %collective-permute-done.9, bf16[3072,1024]{1,0:T(8,128)(2,1)} %get-tuple-element.61, bf16[3072,4096]{1,0:T(8,128)(2,1)} %get-tuple-element.75), kind=kOutput, calls=%fused_computation.137 | convolution fusion | flops 25782386688 | bytes 65011712 | tf_op jit(solution)/shard_map/dot_general | solution.py:16
  1085.0 12.2 convolution_convert_fusion.9
  1101.2 10.1 convolution_convert_fusion.8
  1111.5 2.3 pad_maximum_fusion
  1114.4 7.2 y_finish.5
  1123.1 11.0 fusion.77
  1134.3 13.2 collective-permute-done.18
  1149.4 4.5 fusion.47
  1155.0 14.2 %fusion.76 = (bf16[1024,1280]{1,0:T(8,128)(2,1)S(1)}, f32[1024,1280]{1,0:T(8,128)}) fusion(bf16[1024,1280]{1,0:T(8,128)(2,1)} %collective-permute-done.14, bf16[3072,1024]{1,0:T(8,128)(2,1)S(1)} %bitcast.77, bf16[3072,1280]{1,0:T(8,128)(2,1)} %kv_finish.1), kind=kOutput, calls=%fused_computation.138 | convolution fusion | flops 8056995840 | bytes 24641536 | tf_op jit(solution)/shard_map/dot_general | solution.py:16
  1173.0 34.6 %collective-permute-done.21.peer_ref = bf16[1024,2048]{1,0:T(8,128)(2,1)} collective-permute-done((bf16[1024,2048]{1,0:T(8,128)(2,1)}, bf16[1024,2048]{1,0:T(8,128)(2,1)}, u32[]{:S(2)}, u32[]{:S(2)}) %collective-permute-start.21) | collective-permute-done | bytes 4194336 | tf_op jit(solution)/shard_map/ppermute | solution.py:280
  1209.1 12.4 norm_finish.3
  1221.5 76.0 %collective-permute-done.20.peer_ref = bf16[1024,2048]{1,0:T(8,128)(2,1)} collective-permute-done((bf16[1024,2048]{1,0:T(8,128)(2,1)}, bf16[1024,2048]{1,0:T(8,128)(2,1)}, u32[]{:S(2)}, u32[]{:S(2)}) %collective-permute-start.20) | collective-permute-done | bytes 4194336 | tf_op jit(solution)/shard_map/ppermute | solution.py:280
  1298.8 12.1 norm_finish.4
  1317.0 3.7 fusion.44
  1320.7 2.3 pad_maximum_fusion.1
  1323.0 4.5 collective-permute-done.15
  1328.3 1.7 fusion.61
  1331.7 55.0 %collective-permute-done.17.peer_ref = bf16[1024,2048]{1,0:T(8,128)(2,1)} collective-permute-done((bf16[1024,2048]{1,0:T(8,128)(2,1)}, bf16[1024,2048]{1,0:T(8,128)(2,1)}, u32[]{:S(2)}, u32[]{:S(2)}) %collective-permute-start.17) | collective-permute-done | bytes 4194336 | tf_op jit(solution)/shard_map/ppermute | solution.py:280
  1386.7 12.5 norm_finish.5
  1399.9 12.6 all-reduce
  (158 shorter events, 54.3 us)
Async XLA Ops:
  7.2 4.7 copy-start.15
  7.2 44.4 %all-gather.9.cloned.1.call-start = ((), (), s32[]{:S(2)}) async-start(), calls=%async_computation.1 | async-start | bytes 4718592 | tf_op jit(solution)/shard_map/all_gather | solution.py:284
  7.9 78.0 %all-gather.7.cloned.1.call-start = ((), (), s32[]{:S(2)}) async-start(), calls=%async_computation | async-start | bytes 5898240 | tf_op jit(solution)/shard_map/all_gather | solution.py:283
  10.0 232.4 %all-gather.11.cloned.1.call-start = ((), (), s32[]{:S(2)}) async-start(), calls=%async_computation.2 | async-start | bytes 18874368 | tf_op jit(solution)/shard_map/all_gather | solution.py:285
  10.7 292.6 %all-gather.13.cloned.1.call-start = ((), (), s32[]{:S(2)}) async-start(), calls=%async_computation.3 | async-start | bytes 18874368 | tf_op jit(solution)/shard_map/all_gather | solution.py:286
  11.3 362.1 %all-gather.15.cloned.1.call-start = ((), (), s32[]{:S(2)}) async-start(), calls=%async_computation.4 | async-start | bytes 18874368 | tf_op jit(solution)/shard_map/all_gather | solution.py:287
  223.5 10.7 copy-start.17
  373.4 24.4 %copy-start.16 = (bf16[4096,2048]{1,0:T(8,128)(2,1)S(1)}, bf16[4096,2048]{1,0:T(8,128)(2,1)}, u32[]{:S(2)}) copy-start(bf16[4096,2048]{1,0:T(8,128)(2,1)} %all-gather.15.cloned.1.call-done) | copy-start | bytes 50331652
  420.4 33.9 %copy-start.1 = (f32[3072,256]{1,0:T(8,128)S(1)}, f32[3072,256]{1,0:T(8,128)}, u32[]{:S(2)}) copy-start(f32[3072,256]{1,0:T(8,128)} %get-tuple-element.65.own_ref) | copy-start | bytes 9437188
  420.4 35.4 %copy-start.18 = (u32[16]{0:T(128)S(1)}, u32[16]{0:T(128)}, u32[]{:S(2)}) copy-start(u32[16]{0:T(128)} %constant.33) | copy-start | bytes 196
  453.9 106.2 %collective-permute-start = (bf16[4096,1024]{1,0:T(8,128)(2,1)}, bf16[4096,1024]{1,0:T(8,128)(2,1)}, u32[]{:S(2)}, u32[]{:S(2)}) collective-permute-start(bf16[4096,1024]{1,0:T(8,128)(2,1)} %convolution_convert_fusion.6), channel_id=1, source_target_pairs={{0,1},{1,0},{2,3},{3,2},{4,5},{5,4},{6,7},{7,6},{8,9},{9,8},{10,11... | collective-permute-start | bytes 25165832 | tf_op jit(solution)/shard_map/ppermute | solution.py:214
  454.3 70.2 %collective-permute-start.1 = (f32[3072,256]{1,0:T(8,128)S(1)}, f32[3072,256]{1,0:T(8,128)}, u32[]{:S(2)}, u32[]{:S(2)}) collective-permute-start(f32[3072,256]{1,0:T(8,128)S(1)} %copy-done.1), channel_id=1, source_target_pairs={{0,8},{8,0},{1,9},{9,1},{2,10},{10,2},{3,11},{11,3},{4,12},{12,4},... | collective-permute-start | bytes 9437192 | tf_op jit(solution)/shard_map/ppermute | solution.py:280
  524.5 35.5 %slice-start.6 = ((s8[6291456]{0:T(1024)(128)(4,1)}), s8[2097152]{0:T(1024)(128)(4,1)S(1)}, s32[]{:S(2)}) async-start(s8[6291456]{0:T(1024)(128)(4,1)} %bitcast.78), calls=%async_computation.11 | async-start | bytes 4194304
  533.8 26.3 %slice-start.7 = ((s8[6291456]{0:T(1024)(128)(4,1)}), s8[4194304]{0:T(1024)(128)(4,1)S(1)}, s32[]{:S(2)}) async-start(s8[6291456]{0:T(1024)(128)(4,1)} %bitcast.78), calls=%async_computation.12 | async-start | bytes 8388608
  533.8 378.3 %collective-permute-start.6 = (bf16[1024,2048]{1,0:T(8,128)(2,1)}, bf16[1024,2048]{1,0:T(8,128)(2,1)}, u32[]{:S(2)}, u32[]{:S(2)}) collective-permute-start(bf16[1024,2048]{1,0:T(8,128)(2,1)} %add_convert_fusion.5.own_ref), channel_id=1, source_target_pairs={{0,8},{8,0},{1,9},{9,1},{2,10},{10,2},{3,11},{11,3},{4,12},{12,4},... | collective-permute-start | bytes 12582920 | tf_op jit(solution)/shard_map/ppermute | solution.py:280
  535.3 384.0 %collective-permute-start.5 = (bf16[1024,2048]{1,0:T(8,128)(2,1)}, bf16[1024,2048]{1,0:T(8,128)(2,1)}, u32[]{:S(2)}, u32[]{:S(2)}) collective-permute-start(bf16[1024,2048]{1,0:T(8,128)(2,1)} %add_convert_fusion.4.own_ref), channel_id=1, source_target_pairs={{0,8},{8,0},{1,9},{9,1},{2,10},{10,2},{3,11},{11,3},{4,12},{12,4},... | collective-permute-start | bytes 12582920 | tf_op jit(solution)/shard_map/ppermute | solution.py:280
  596.0 174.7 %collective-permute-start.2 = (bf16[2048,512]{1,0:T(8,128)(2,1)}, bf16[2048,512]{1,0:T(8,128)(2,1)}, u32[]{:S(2)}, u32[]{:S(2)}) collective-permute-start(bf16[2048,512]{1,0:T(8,128)(2,1)} %pad_maximum_fusion.3), channel_id=1, source_target_pairs={{0,2},{1,3},{2,0},{3,1},{4,6},{5,7},{6,4},{7,5},{8,10},{9,11},{10,... | collective-permute-start | bytes 6291464 | tf_op jit(solution)/shard_map/ppermute | solution.py:214
  597.6 173.2 %collective-permute-start.3 = (bf16[2048,512]{1,0:T(8,128)(2,1)}, bf16[2048,512]{1,0:T(8,128)(2,1)}, u32[]{:S(2)}, u32[]{:S(2)}) collective-permute-start(bf16[2048,512]{1,0:T(8,128)(2,1)} %concatenate.72), channel_id=1, source_target_pairs={{0,4},{1,5},{2,6},{3,7},{4,0},{5,1},{6,2},{7,3},{8,12},{9,13},{10,... | collective-permute-start | bytes 6291464 | tf_op jit(solution)/shard_map/ppermute | solution.py:214
  709.7 48.6 %slice-start = ((s8[7864320]{0:T(1024)(128)(4,1)}), s8[4194304]{0:T(1024)(128)(4,1)S(1)}, s32[]{:S(2)}) async-start(s8[7864320]{0:T(1024)(128)(4,1)} %bitcast.66), calls=%async_computation.5 | async-start | bytes 8388608
  733.9 24.3 %slice-start.1 = ((s8[7864320]{0:T(1024)(128)(4,1)}), s8[3670016]{0:T(1024)(128)(4,1)S(1)}, s32[]{:S(2)}) async-start(s8[7864320]{0:T(1024)(128)(4,1)} %bitcast.66), calls=%async_computation.6 | async-start | bytes 7340032
  733.9 24.3 %copy-start.14 = (pred[1280]{0:T(1024)(128)(4,1)S(1)}, pred[1280]{0:T(1024)(128)(4,1)}, u32[]{:S(2)}) copy-start(pred[1280]{0:T(1024)(128)(4,1)} %fusion.70) | copy-start | bytes 3844
  807.4 69.3 %collective-permute-start.4 = (bf16[1024,4096]{1,0:T(8,128)(2,1)}, bf16[1024,4096]{1,0:T(8,128)(2,1)}, u32[]{:S(2)}, u32[]{:S(2)}) collective-permute-start(bf16[1024,4096]{1,0:T(8,128)(2,1)} %convolution_convert_fusion.5), channel_id=1, source_target_pairs={{0,1},{1,0},{2,3},{3,2},{4,5},{5,4},{6,7},{7,6},{8,9},{9,8},{10,11... | collective-permute-start | bytes 25165832 | tf_op jit(solution)/shard_map/ppermute | solution.py:214
  831.7 38.4 %collective-permute-start.30 = (bf16[2048,256]{1,0:T(8,128)(2,1)S(1)}, bf16[2048,256]{1,0:T(8,128)(2,1)S(1)}, u32[]{:S(2)}, u32[]{:S(2)}) collective-permute-start(bf16[2048,256]{1,0:T(8,128)(2,1)S(1)} %get-tuple-element.123), channel_id=1, source_target_pairs={{0,4},{1,5},{2,6},{3,7},{4,0},{5,1},{6,2},{7,3},{8,12},{9,13},{10,... | collective-permute-start | bytes 3145736 | tf_op jit(solution)/shard_map/ppermute | solution.py:214
  833.1 38.5 %collective-permute-start.31 = (bf16[2048,256]{1,0:T(8,128)(2,1)S(1)}, bf16[2048,256]{1,0:T(8,128)(2,1)}, u32[]{:S(2)}, u32[]{:S(2)}) collective-permute-start(bf16[2048,256]{1,0:T(8,128)(2,1)S(1)} %get-tuple-element.122), channel_id=1, source_target_pairs={{0,2},{1,3},{2,0},{3,1},{4,6},{5,7},{6,4},{7,5},{8,10},{9,11},{10,... | collective-permute-start | bytes 3145736 | tf_op jit(solution)/shard_map/ppermute | solution.py:214
  870.1 243.7 %collective-permute-start.10 = (bf16[1024,2048]{1,0:T(8,128)(2,1)}, bf16[1024,2048]{1,0:T(8,128)(2,1)}, u32[]{:S(2)}, u32[]{:S(2)}) collective-permute-start(bf16[1024,2048]{1,0:T(8,128)(2,1)} %add_convert_fusion.3.own_ref), channel_id=1, source_target_pairs={{0,8},{8,0},{1,9},{9,1},{2,10},{10,2},{3,11},{11,3},{4,12},{12,4},... | collective-permute-start | bytes 12582920 | tf_op jit(solution)/shard_map/ppermute | solution.py:280
  926.5 33.6 %copy-start = (f32[2048,256]{1,0:T(8,128)S(1)}, f32[2048,256]{1,0:T(8,128)}, u32[]{:S(2)}) copy-start(f32[2048,256]{1,0:T(8,128)} %get-tuple-element.113) | copy-start | bytes 6291460
  960.1 89.9 %collective-permute-start.9 = (bf16[1024,4096]{1,0:T(8,128)(2,1)}, bf16[1024,4096]{1,0:T(8,128)(2,1)}, u32[]{:S(2)}, u32[]{:S(2)}) collective-permute-start(bf16[1024,4096]{1,0:T(8,128)(2,1)} %convolution_convert_fusion.4), channel_id=1, source_target_pairs={{0,1},{1,0},{2,3},{3,2},{4,5},{5,4},{6,7},{7,6},{8,9},{9,8},{10,11... | collective-permute-start | bytes 25165832 | tf_op jit(solution)/shard_map/ppermute | solution.py:214
  964.1 59.0 %slice-start.2 = ((s8[7864320]{0:T(1024)(128)(4,1)}), s8[4194304]{0:T(1024)(128)(4,1)S(1)}, s32[]{:S(2)}) async-start(s8[7864320]{0:T(1024)(128)(4,1)} %bitcast.68), calls=%async_computation.7 | async-start | bytes 8388608
  966.3 56.8 %slice-start.3 = ((s8[7864320]{0:T(1024)(128)(4,1)}), s8[3670016]{0:T(1024)(128)(4,1)S(1)}, s32[]{:S(2)}) async-start(s8[7864320]{0:T(1024)(128)(4,1)} %bitcast.68), calls=%async_computation.8 | async-start | bytes 7340032
  966.3 48.1 %collective-permute-start.7 = (bf16[512,2048]{1,0:T(8,128)(2,1)S(1)}, bf16[512,2048]{1,0:T(8,128)(2,1)S(1)}, u32[]{:S(2)}, u32[]{:S(2)}) collective-permute-start(bf16[512,2048]{1,0:T(8,128)(2,1)S(1)} %pad_maximum_fusion.4), channel_id=1, source_target_pairs={{0,2},{1,3},{2,0},{3,1},{4,6},{5,7},{6,4},{7,5},{8,10},{9,11},{10,... | collective-permute-start | bytes 6291464 | tf_op jit(solution)/shard_map/ppermute | solution.py:214
  967.8 47.8 %collective-permute-start.8 = (bf16[512,2048]{1,0:T(8,128)(2,1)S(1)}, bf16[512,2048]{1,0:T(8,128)(2,1)S(1)}, u32[]{:S(2)}, u32[]{:S(2)}) collective-permute-start(bf16[512,2048]{1,0:T(8,128)(2,1)S(1)} %concatenate.73), channel_id=1, source_target_pairs={{0,4},{1,5},{2,6},{3,7},{4,0},{5,1},{6,2},{7,3},{8,12},{9,13},{10,... | collective-permute-start | bytes 6291464 | tf_op jit(solution)/shard_map/ppermute | solution.py:214
  1021.2 24.6 %collective-permute-start.26 = (bf16[256,2048]{1,0:T(8,128)(2,1)}, bf16[256,2048]{1,0:T(8,128)(2,1)S(1)}, u32[]{:S(2)}, u32[]{:S(2)}) collective-permute-start(bf16[256,2048]{1,0:T(8,128)(2,1)} %get-tuple-element.121), channel_id=1, source_target_pairs={{0,4},{1,5},{2,6},{3,7},{4,0},{5,1},{6,2},{7,3},{8,12},{9,13},{10,... | collective-permute-start | bytes 3145736 | tf_op jit(solution)/shard_map/ppermute | solution.py:214
  1021.8 24.5 %collective-permute-start.27 = (bf16[256,2048]{1,0:T(8,128)(2,1)}, bf16[256,2048]{1,0:T(8,128)(2,1)}, u32[]{:S(2)}, u32[]{:S(2)}) collective-permute-start(bf16[256,2048]{1,0:T(8,128)(2,1)} %get-tuple-element.120), channel_id=1, source_target_pairs={{0,2},{1,3},{2,0},{3,1},{4,6},{5,7},{6,4},{7,5},{8,10},{9,11},{10,... | collective-permute-start | bytes 3145736 | tf_op jit(solution)/shard_map/ppermute | solution.py:214
  1085.0 12.2 copy-start.2
  1097.2 24.4 %collective-permute-start.11 = (bf16[1024,1024]{1,0:T(8,128)(2,1)}, bf16[1024,1024]{1,0:T(8,128)(2,1)}, u32[]{:S(2)}, u32[]{:S(2)}) collective-permute-start(bf16[1024,1024]{1,0:T(8,128)(2,1)} %convolution_convert_fusion.9), channel_id=1, source_target_pairs={{0,1},{1,0},{2,3},{3,2},{4,5},{5,4},{6,7},{7,6},{8,9},{9,8},{10,11... | collective-permute-start | bytes 6291464 | tf_op jit(solution)/shard_map/ppermute | solution.py:214
  1097.3 3.9 slice-start.8
  1097.5 3.7 slice-start.9
  1099.2 48.3 %collective-permute-start.18 = (bf16[512,2048]{1,0:T(8,128)(2,1)}, bf16[512,2048]{1,0:T(8,128)(2,1)}, u32[]{:S(2)}, u32[]{:S(2)}) collective-permute-start(bf16[512,2048]{1,0:T(8,128)(2,1)} %pad_maximum_fusion.5), channel_id=1, source_target_pairs={{0,2},{1,3},{2,0},{3,1},{4,6},{5,7},{6,4},{7,5},{8,10},{9,11},{10,... | collective-permute-start | bytes 6291464 | tf_op jit(solution)/shard_map/ppermute | solution.py:214
  1100.5 47.8 %collective-permute-start.19 = (bf16[512,2048]{1,0:T(8,128)(2,1)S(1)}, bf16[512,2048]{1,0:T(8,128)(2,1)}, u32[]{:S(2)}, u32[]{:S(2)}) collective-permute-start(bf16[512,2048]{1,0:T(8,128)(2,1)S(1)} %concatenate.76), channel_id=1, source_target_pairs={{0,4},{1,5},{2,6},{3,7},{4,0},{5,1},{6,2},{7,3},{8,12},{9,13},{10,... | collective-permute-start | bytes 6291464 | tf_op jit(solution)/shard_map/ppermute | solution.py:214
  1111.3 42.6 %collective-permute-start.14 = (bf16[1024,1280]{1,0:T(8,128)(2,1)}, bf16[1024,1280]{1,0:T(8,128)(2,1)}, u32[]{:S(2)}, u32[]{:S(2)}) collective-permute-start(bf16[1024,1280]{1,0:T(8,128)(2,1)} %convolution_convert_fusion.8), channel_id=1, source_target_pairs={{0,1},{1,0},{2,3},{3,2},{4,5},{5,4},{6,7},{7,6},{8,9},{9,8},{10,11... | collective-permute-start | bytes 7864328 | tf_op jit(solution)/shard_map/ppermute | solution.py:214
  1113.8 93.8 %collective-permute-start.21 = (bf16[1024,2048]{1,0:T(8,128)(2,1)}, bf16[1024,2048]{1,0:T(8,128)(2,1)}, u32[]{:S(2)}, u32[]{:S(2)}) collective-permute-start(bf16[1024,2048]{1,0:T(8,128)(2,1)} %add_convert_fusion.2.own_ref), channel_id=1, source_target_pairs={{0,8},{8,0},{1,9},{9,1},{2,10},{10,2},{3,11},{11,3},{4,12},{12,4},... | collective-permute-start | bytes 12582920 | tf_op jit(solution)/shard_map/ppermute | solution.py:280
  1121.6 175.9 %collective-permute-start.20 = (bf16[1024,2048]{1,0:T(8,128)(2,1)}, bf16[1024,2048]{1,0:T(8,128)(2,1)}, u32[]{:S(2)}, u32[]{:S(2)}) collective-permute-start(bf16[1024,2048]{1,0:T(8,128)(2,1)} %add_convert_fusion.1.own_ref), channel_id=1, source_target_pairs={{0,8},{8,0},{1,9},{9,1},{2,10},{10,2},{3,11},{11,3},{4,12},{12,4},... | collective-permute-start | bytes 12582920 | tf_op jit(solution)/shard_map/ppermute | solution.py:280
  1134.1 38.0 %copy-start.4 = (f32[1024,1024]{1,0:T(8,128)}, f32[1024,1024]{1,0:T(8,128)S(1)}, u32[]{:S(2)}) copy-start(f32[1024,1024]{1,0:T(8,128)S(1)} %get-tuple-element.105) | copy-start | bytes 12582916
  1134.1 20.8 %slice-start.4 = ((s8[6291456]{0:T(1024)(128)(4,1)}), s8[4194304]{0:T(1024)(128)(4,1)S(1)}, s32[]{:S(2)}) async-start(s8[6291456]{0:T(1024)(128)(4,1)} %bitcast.76), calls=%async_computation.9 | async-start | bytes 8388608
  1134.3 20.7 %slice-start.5 = ((s8[6291456]{0:T(1024)(128)(4,1)}), s8[2097152]{0:T(1024)(128)(4,1)S(1)}, s32[]{:S(2)}) async-start(s8[6291456]{0:T(1024)(128)(4,1)} %bitcast.76), calls=%async_computation.10 | async-start | bytes 4194304
  1147.5 239.1 %collective-permute-start.17 = (bf16[1024,2048]{1,0:T(8,128)(2,1)}, bf16[1024,2048]{1,0:T(8,128)(2,1)}, u32[]{:S(2)}, u32[]{:S(2)}) collective-permute-start(bf16[1024,2048]{1,0:T(8,128)(2,1)} %add_convert_fusion.own_ref), channel_id=1, source_target_pairs={{0,8},{8,0},{1,9},{9,1},{2,10},{10,2},{3,11},{11,3},{4,12},{12,4},... | collective-permute-start | bytes 12582920 | tf_op jit(solution)/shard_map/ppermute | solution.py:280
  1148.3 21.8 %collective-permute-start.12 = (bf16[512,512]{1,0:T(8,128)(2,1)S(1)}, bf16[512,512]{1,0:T(8,128)(2,1)S(1)}, u32[]{:S(2)}, u32[]{:S(2)}) collective-permute-start(bf16[512,512]{1,0:T(8,128)(2,1)S(1)} %pad_maximum_fusion.12), channel_id=1, source_target_pairs={{0,2},{1,3},{2,0},{3,1},{4,6},{5,7},{6,4},{7,5},{8,10},{9,11},{10,... | collective-permute-start | bytes 1572872 | tf_op jit(solution)/shard_map/ppermute | solution.py:214
  1153.9 17.3 %collective-permute-start.13 = (bf16[512,512]{1,0:T(8,128)(2,1)S(1)}, bf16[512,512]{1,0:T(8,128)(2,1)S(1)}, u32[]{:S(2)}, u32[]{:S(2)}) collective-permute-start(bf16[512,512]{1,0:T(8,128)(2,1)S(1)} %concatenate.74), channel_id=1, source_target_pairs={{0,4},{1,5},{2,6},{3,7},{4,0},{5,1},{6,2},{7,3},{8,12},{9,13},{10,... | collective-permute-start | bytes 1572872 | tf_op jit(solution)/shard_map/ppermute | solution.py:214
  1169.2 3.8 copy-start.5
  1170.2 37.4 %copy-start.10 = (bf16[512,512]{1,0:T(8,128)(2,1)}, bf16[512,512]{1,0:T(8,128)(2,1)S(1)}, u32[]{:S(2)}) copy-start(bf16[512,512]{1,0:T(8,128)(2,1)S(1)} %collective-permute-done.12) | copy-start | bytes 1572868
  1170.2 146.8 %collective-permute-start.28 = (bf16[256,2048]{1,0:T(8,128)(2,1)}, bf16[256,2048]{1,0:T(8,128)(2,1)S(1)}, u32[]{:S(2)}, u32[]{:S(2)}) collective-permute-start(bf16[256,2048]{1,0:T(8,128)(2,1)} %get-tuple-element.119), channel_id=1, source_target_pairs={{0,4},{1,5},{2,6},{3,7},{4,0},{5,1},{6,2},{7,3},{8,12},{9,13},{10,... | collective-permute-start | bytes 3145736 | tf_op jit(solution)/shard_map/ppermute | solution.py:214
  1171.1 36.5 %copy-start.11 = (bf16[512,512]{1,0:T(8,128)(2,1)}, bf16[512,512]{1,0:T(8,128)(2,1)S(1)}, u32[]{:S(2)}) copy-start(bf16[512,512]{1,0:T(8,128)(2,1)S(1)} %collective-permute-done.13) | copy-start | bytes 1572868
  1171.1 145.8 %collective-permute-start.29 = (bf16[256,2048]{1,0:T(8,128)(2,1)S(1)}, bf16[256,2048]{1,0:T(8,128)(2,1)S(1)}, u32[]{:S(2)}, u32[]{:S(2)}) collective-permute-start(bf16[256,2048]{1,0:T(8,128)(2,1)S(1)} %get-tuple-element.118), channel_id=1, source_target_pairs={{0,2},{1,3},{2,0},{3,1},{4,6},{5,7},{6,4},{7,5},{8,10},{9,11},{10,... | collective-permute-start | bytes 3145736 | tf_op jit(solution)/shard_map/ppermute | solution.py:214
  1207.6 104.5 %collective-permute-start.24 = (bf16[512,256]{1,0:T(8,128)(2,1)}, bf16[512,256]{1,0:T(8,128)(2,1)S(1)}, u32[]{:S(2)}, u32[]{:S(2)}) collective-permute-start(bf16[512,256]{1,0:T(8,128)(2,1)} %get-tuple-element.137), channel_id=1, source_target_pairs={{0,4},{1,5},{2,6},{3,7},{4,0},{5,1},{6,2},{7,3},{8,12},{9,13},{10,... | collective-permute-start | bytes 786440 | tf_op jit(solution)/shard_map/ppermute | solution.py:214
  1297.5 15.4 %collective-permute-start.25 = (bf16[512,256]{1,0:T(8,128)(2,1)}, bf16[512,256]{1,0:T(8,128)(2,1)}, u32[]{:S(2)}, u32[]{:S(2)}) collective-permute-start(bf16[512,256]{1,0:T(8,128)(2,1)} %get-tuple-element.136), channel_id=1, source_target_pairs={{0,2},{1,3},{2,0},{3,1},{4,6},{5,7},{6,4},{7,5},{8,10},{9,11},{10,... | collective-permute-start | bytes 786440 | tf_op jit(solution)/shard_map/ppermute | solution.py:214
  1312.1 15.3 %collective-permute-start.15 = (bf16[512,640]{1,0:T(8,128)(2,1)S(1)}, bf16[512,640]{1,0:T(8,128)(2,1)S(1)}, u32[]{:S(2)}, u32[]{:S(2)}) collective-permute-start(bf16[512,640]{1,0:T(8,128)(2,1)S(1)} %pad_maximum_fusion.9), channel_id=1, source_target_pairs={{0,2},{1,3},{2,0},{3,1},{4,6},{5,7},{6,4},{7,5},{8,10},{9,11},{10,... | collective-permute-start | bytes 1966088 | tf_op jit(solution)/shard_map/ppermute | solution.py:214
  1312.9 15.0 %collective-permute-start.16 = (bf16[512,640]{1,0:T(8,128)(2,1)}, bf16[512,640]{1,0:T(8,128)(2,1)S(1)}, u32[]{:S(2)}, u32[]{:S(2)}) collective-permute-start(bf16[512,640]{1,0:T(8,128)(2,1)} %concatenate.75), channel_id=1, source_target_pairs={{0,4},{1,5},{2,6},{3,7},{4,0},{5,1},{6,2},{7,3},{8,12},{9,13},{10,... | collective-permute-start | bytes 1966088 | tf_op jit(solution)/shard_map/ppermute | solution.py:214
  1328.3 58.3 %copy-start.8 = (bf16[512,640]{1,0:T(8,128)(2,1)}, bf16[512,640]{1,0:T(8,128)(2,1)S(1)}, u32[]{:S(2)}) copy-start(bf16[512,640]{1,0:T(8,128)(2,1)S(1)} %collective-permute-done.16) | copy-start | bytes 1966084
  1330.0 83.1 %collective-permute-start.22 = (bf16[256,640]{1,0:T(8,128)(2,1)S(1)}, bf16[256,640]{1,0:T(8,128)(2,1)S(1)}, u32[]{:S(2)}, u32[]{:S(2)}) collective-permute-start(bf16[256,640]{1,0:T(8,128)(2,1)S(1)} %get-tuple-element.133), channel_id=1, source_target_pairs={{0,4},{1,5},{2,6},{3,7},{4,0},{5,1},{6,2},{7,3},{8,12},{9,13},{10,... | collective-permute-start | bytes 983048 | tf_op jit(solution)/shard_map/ppermute | solution.py:214
  1330.8 82.3 %collective-permute-start.23 = (bf16[256,640]{1,0:T(8,128)(2,1)S(1)}, bf16[256,640]{1,0:T(8,128)(2,1)S(1)}, u32[]{:S(2)}, u32[]{:S(2)}) collective-permute-start(bf16[256,640]{1,0:T(8,128)(2,1)S(1)} %get-tuple-element.132), channel_id=1, source_target_pairs={{0,2},{1,3},{2,0},{3,1},{4,6},{5,7},{6,4},{7,5},{8,10},{9,11},{10,... | collective-permute-start | bytes 983048 | tf_op jit(solution)/shard_map/ppermute | solution.py:214
  1386.7 12.5 copy-start.12
  1386.7 12.5 copy-start.13
  1386.7 26.5 %copy-start.7 = (bf16[512,640]{1,0:T(8,128)(2,1)S(1)}, bf16[512,640]{1,0:T(8,128)(2,1)}, u32[]{:S(2)}) copy-start(bf16[512,640]{1,0:T(8,128)(2,1)} %copy-done.6) | copy-start | bytes 1966084
  1386.7 26.5 %copy-start.9 = (bf16[512,640]{1,0:T(8,128)(2,1)S(1)}, bf16[512,640]{1,0:T(8,128)(2,1)}, u32[]{:S(2)}) copy-start(bf16[512,640]{1,0:T(8,128)(2,1)} %copy-done.8) | copy-start | bytes 1966084
  (2 other events, 2.2 us)
Sparse Core Ops, SparseCore 0:
  9.8 36.3 all-gather.8
  48.7 37.2 all-gather.6
  87.8 85.9 all-gather.10
  175.5 85.9 all-gather.12
  263.2 89.2 all-gather.14
